TPU v7x, 16 devices: a whole 2x2x2 slice. The times are simulated.
16 devices in a mesh: dp: 4 (over z, y), fsdp: 4 (over x, core).
Axes of the slice: x: 2, y: 2, z: 2, core: 2. Of those that a mesh axis runs over, the one named last changes fastest.
Arguments:
- u_in: bfloat16 [16, 512, 1536], P(('dp', 'fsdp'))
- grad_out: bfloat16 [16, 512, 1536], P(('dp', 'fsdp'))
- norm_w: bfloat16 [2, 1536], P(None, 'fsdp')
- w_in: bfloat16 [2, 1536, 6448], P(None, 'fsdp')
- conv_w: bfloat16 [2, 4, 3328], P(None, None, 'fsdp')
- conv_b: bfloat16 [2, 3328], P(None, 'fsdp')
- dt_bias: float32 [2, 48], P(None, 'fsdp')
- a_log: float32 [2, 48], P(None, 'fsdp')
- d_skip: float32 [2, 48], P(None, 'fsdp')
- gate_w: bfloat16 [2, 3072], P(None, 'fsdp')
- w_out: bfloat16 [2, 3072, 1536], P(None, 'fsdp')
Outputs:
- output 1: bfloat16 [16, 512, 1536], P(('dp', 'fsdp'))
- output 2: bfloat16 [16, 512, 1536], P(('dp', 'fsdp'))
- output 3: float32 [2, 1536], P(None, 'fsdp')
- output 4: float32 [2, 1536, 6448], P(None, 'fsdp')
- output 5: float32 [2, 4, 3328], P(None, None, 'fsdp')
- output 6: float32 [2, 3328], P(None, 'fsdp')
- output 7: float32 [2, 48], P(None, 'fsdp')
- output 8: float32 [2, 48], P(None, 'fsdp')
- output 9: float32 [2, 48], P(None, 'fsdp')
- output 10: float32 [2, 3072], P(None, 'fsdp')
- output 11: float32 [2, 3072, 1536], P(None, 'fsdp')
All inputs are finite; a program needn't handle non-finite values.
Results may differ from a plain program's by a relative error of at most 0.02.
Values are sent between devices in bfloat16 or wider.
A program may use at most 1 GiB of HBM per device.

v0:
```python
import jax
import jax.numpy as jnp
from jax import lax
from jax.sharding import PartitionSpec as P

CHUNK_LEN = 256
STATE_DIM = 128
NORM_EPS = 1e-5
GATHER_AXES = (0, 0, 1, 0, 0, 0, 0, 0, 0)


def pre_norm(u_rows, norm_w):
    rows_f = u_rows.astype(jnp.float32)
    inv_rms = lax.rsqrt(jnp.mean(jnp.square(rows_f), axis=-1, keepdims=True) + NORM_EPS)
    return (rows_f * inv_rms * norm_w.astype(jnp.float32)).astype(jnp.bfloat16)


def ssd_chunks(x_heads, dt_heads, a_heads, b_mat, c_mat):
    n_batch, seq_len, n_heads, head_dim = x_heads.shape
    n_groups = b_mat.shape[2]
    per_group = n_heads // n_groups
    n_chunks = seq_len // CHUNK_LEN
    block_shape = (n_batch, n_chunks, CHUNK_LEN, n_groups)
    x_dt = (x_heads * dt_heads[..., None]).reshape(block_shape + (per_group, head_dim))
    cum_a = jnp.cumsum(a_heads.reshape(block_shape + (per_group,)), axis=2)
    b_chunk = b_mat.reshape(block_shape + (STATE_DIM,))
    c_chunk = c_mat.reshape(block_shape + (STATE_DIM,))
    scores = jnp.einsum('bcqgn,bcsgn->bcgqs', c_chunk, b_chunk, preferred_element_type=jnp.float32)
    cum_t = jnp.moveaxis(cum_a, 2, -1)
    log_gap = cum_t[..., :, None] - cum_t[..., None, :]
    causal = jnp.arange(CHUNK_LEN)[:, None] >= jnp.arange(CHUNK_LEN)[None, :]
    decay_mat = jnp.where(causal, jnp.exp(jnp.where(causal, log_gap, 0.0)), 0.0)
    y_diag = jnp.einsum('bcgrqs,bcsgrp->bcqgrp', scores[:, :, :, None] * decay_mat, x_dt, preferred_element_type=jnp.float32)
    end_decay = jnp.exp(cum_a[:, :, -1:] - cum_a)
    states = jnp.einsum('bcsgn,bcsgrp->bcgrpn', b_chunk, x_dt * end_decay[..., None], preferred_element_type=jnp.float32)
    totals = cum_a[:, :, -1]
    incl_sum = jnp.cumsum(totals, axis=1)
    excl_sum = incl_sum - totals
    chunk_gap = jnp.moveaxis(excl_sum, 1, -1)[..., :, None] - jnp.moveaxis(incl_sum, 1, -1)[..., None, :]
    earlier = jnp.arange(n_chunks)[:, None] > jnp.arange(n_chunks)[None, :]
    carry_mat = jnp.where(earlier, jnp.exp(jnp.where(earlier, chunk_gap, 0.0)), 0.0)
    prev_state = jnp.einsum('bgrij,bjgrpn->bigrpn', carry_mat, states, preferred_element_type=jnp.float32)
    y_off = jnp.einsum('bcqgn,bcgrpn->bcqgrp', c_chunk, prev_state, preferred_element_type=jnp.float32) * jnp.exp(cum_a)[..., None]
    return (y_diag + y_off).reshape(x_heads.shape)


def mixer_core(proj_out, conv_w, conv_b, dt_bias, a_log, d_skip, gate_w):
    n_batch, seq_len, _ = proj_out.shape
    d_inner = gate_w.shape[0]
    conv_dim = conv_b.shape[0]
    n_heads = dt_bias.shape[0]
    n_taps = conv_w.shape[0]
    n_groups = (conv_dim - d_inner) // (2 * STATE_DIM)
    group_w = n_groups * STATE_DIM
    padded = jnp.pad(proj_out[:, :, d_inner:d_inner + conv_dim], ((0, 0), (n_taps - 1, 0), (0, 0)))
    conv_out = conv_b.astype(jnp.float32) + sum(padded[:, tap:tap + seq_len] * conv_w[tap].astype(jnp.float32) for tap in range(n_taps))
    xbc_act = jax.nn.silu(conv_out)
    x_heads = xbc_act[:, :, :d_inner].reshape(n_batch, seq_len, n_heads, d_inner // n_heads)
    b_mat = xbc_act[:, :, d_inner:d_inner + group_w].reshape(n_batch, seq_len, n_groups, STATE_DIM)
    c_mat = xbc_act[:, :, d_inner + group_w:].reshape(n_batch, seq_len, n_groups, STATE_DIM)
    dt_heads = jax.nn.softplus(proj_out[:, :, d_inner + conv_dim:].astype(jnp.float32) + dt_bias)
    y_heads = ssd_chunks(x_heads, dt_heads, dt_heads * -jnp.exp(a_log), b_mat, c_mat) + d_skip[:, None] * x_heads
    z_act = jax.nn.silu(proj_out[:, :, :d_inner].astype(jnp.float32))
    gated_y = y_heads.reshape(n_batch, seq_len, n_groups, -1) * z_act.reshape(n_batch, seq_len, n_groups, -1)
    normed = gated_y * lax.rsqrt(jnp.mean(jnp.square(gated_y), axis=-1, keepdims=True) + NORM_EPS)
    return (normed.reshape(n_batch, seq_len, d_inner) * gate_w.astype(jnp.float32)).astype(jnp.bfloat16)


def layer_forward(u_rows, params):
    norm_w, w_in, conv_w, conv_b, dt_bias, a_log, d_skip, gate_w, w_out = params
    h_norm, norm_pull = jax.vjp(pre_norm, u_rows, norm_w)
    proj_out = jnp.einsum('bld,dk->blk', h_norm, w_in, preferred_element_type=jnp.float32).astype(jnp.bfloat16)
    y_norm, core_pull = jax.vjp(mixer_core, proj_out, conv_w, conv_b, dt_bias, a_log, d_skip, gate_w)
    mixed = jnp.einsum('blk,kd->bld', y_norm, w_out, preferred_element_type=jnp.float32)
    out_rows = (u_rows.astype(jnp.float32) + mixed).astype(jnp.bfloat16)
    return out_rows, (h_norm, y_norm, norm_pull, core_pull)


def layer_backward(d_out, saved, w_in, w_out):
    h_norm, y_norm, norm_pull, core_pull = saved
    g_w_out = jnp.einsum('blk,bld->kd', y_norm, d_out, preferred_element_type=jnp.float32)
    d_ynorm = jnp.einsum('bld,kd->blk', d_out, w_out, preferred_element_type=jnp.float32).astype(jnp.bfloat16)
    d_proj, g_conv_w, g_conv_b, g_dt_bias, g_a_log, g_d_skip, g_gate_w = core_pull(d_ynorm)
    g_w_in = jnp.einsum('bld,blk->dk', h_norm, d_proj, preferred_element_type=jnp.float32)
    d_h = jnp.einsum('blk,dk->bld', d_proj, w_in, preferred_element_type=jnp.float32).astype(jnp.bfloat16)
    d_u_norm, g_norm_w = norm_pull(d_h)
    d_u = (d_out.astype(jnp.float32) + d_u_norm.astype(jnp.float32)).astype(jnp.bfloat16)
    return d_u, (g_norm_w, g_w_in, g_conv_w, g_conv_b, g_dt_bias, g_a_log, g_d_skip, g_gate_w, g_w_out)


def solution(mesh):
    dp_size = mesh.shape['dp']
    fsdp_size = mesh.shape['fsdp']
    act_spec = P(('dp', 'fsdp'), None, None)
    weight_specs = (P(None, 'fsdp'), P(None, 'fsdp', None), P(None, None, 'fsdp'), P(None, 'fsdp'), P(None, 'fsdp'), P(None, 'fsdp'), P(None, 'fsdp'), P(None, 'fsdp'), P(None, 'fsdp', None))

    def per_device(u_loc, g_loc, *pieces):
        batch_tot = u_loc.shape[0] * dp_size * fsdp_size

        def gather_layer(layer):
            return tuple(lax.all_gather(piece[layer], 'fsdp', axis=axis_id, tiled=True) for piece, axis_id in zip(pieces, GATHER_AXES))

        def gather_big(layer):
            w_in = lax.all_gather(pieces[1][layer], 'fsdp', axis=0, tiled=True)
            w_out = lax.all_gather(pieces[8][layer], 'fsdp', axis=0, tiled=True)
            return w_in, w_out

        def reduce_layer(grads):
            out_pieces = []
            for grad, piece, axis_id in zip(grads, pieces, GATHER_AXES):
                part_g = (grad.astype(jnp.float32) / batch_tot).astype(piece.dtype)
                summed = lax.psum_scatter(part_g, 'fsdp', scatter_dimension=axis_id, tiled=True)
                out_pieces.append(lax.psum(summed.astype(jnp.float32), 'dp'))
            return out_pieces

        full_one = gather_layer(0)
        hidden, saved_one = layer_forward(u_loc, full_one)
        full_two = gather_layer(1)
        out_loc, saved_two = layer_forward(hidden, full_two)
        in_two, out_two = gather_big(1)
        d_hidden, grads_two = layer_backward(g_loc, saved_two, in_two, out_two)
        pieces_two = reduce_layer(grads_two)
        in_one, out_one = gather_big(0)
        d_u, grads_one = layer_backward(d_hidden, saved_one, in_one, out_one)
        pieces_one = reduce_layer(grads_one)
        stacked = tuple(jnp.stack([first, second]) for first, second in zip(pieces_one, pieces_two))
        return (out_loc, d_u) + stacked

    return jax.shard_map(per_device, mesh=mesh, in_specs=(act_spec, act_spec) + weight_specs, out_specs=(act_spec, act_spec) + weight_specs, check_vma=False)
```

profile of v0, /device:TPU:0, one launch (start us, length us, event | category | flops | bytes accessed | tf_op | source)
XLA Modules:
  0.0 1759.9 jit_solution(4719253012234196751)
XLA Ops:
  30.0 23.9 %all-gather.3 = bf16[1,4,3328]{1,0,2:T(2,128)(2,1)S(1)} all-gather(bf16[1,4,832]{1,0,2:T(2,128)(2,1)S(1)} %copy.754), channel_id=5, replica_groups=mesh['dp'=4,'fsdp'=4] {'fsdp'}, dimensions={2}, use_global_device_ids=true | all-gather | bytes 33280 | tf_op jit(solution)/shard_map/all_gather | solution.py:101
  53.9 70.1 %fusion.281 = (f32[3328]{0:T(1024)S(1)}, f32[3328]{0:T(1024)S(1)}, f32[3328]{0:T(1024)S(1)}, f32[3328]{0:T(1024)S(1)}) fusion(bf16[1,4,3328]{1,0,2:T(2,128)(2,1)S(1)} %all-gather.3), kind=kLoop, calls=%fused_computation.351 | loop fusion | flops 13312 | bytes 79872 | tf_op jit(solution)/shard_map/jvp()/convert_element_type | solution.py:56
  125.8 13.5 all-reduce.59
  165.7 23.3 %all-gather.12 = bf16[1,4,3328]{1,0,2:T(2,128)(2,1)S(1)} all-gather(bf16[1,4,832]{1,0,2:T(2,128)(2,1)S(1)} %copy.755), channel_id=14, replica_groups=mesh['dp'=4,'fsdp'=4] {'fsdp'}, dimensions={2}, use_global_device_ids=true | all-gather | bytes 33280 | tf_op jit(solution)/shard_map/all_gather | solution.py:101
  189.0 70.8 %fusion.277 = (f32[3328]{0:T(1024)S(1)}, f32[3328]{0:T(1024)S(1)}, f32[3328]{0:T(1024)S(1)}, f32[3328]{0:T(1024)}) fusion(bf16[1,4,3328]{1,0,2:T(2,128)(2,1)S(1)} %all-gather.12), kind=kLoop, calls=%fused_computation.343 | loop fusion | flops 13312 | bytes 79872 | tf_op jit(solution)/shard_map/jvp()/convert_element_type | solution.py:56
  261.7 15.4 fusion.53
  353.2 11.6 fusion.183
  366.0 15.3 fusion.50
  466.2 16.7 fusion.129
  513.3 12.9 fusion.128
  558.6 11.7 copy.638
  597.7 18.1 %fusion.21 = (f32[2,48,256]{2,1,0:T(8,128)S(1)}, f32[2,48,256]{2,1,0:T(8,128)S(1)}, bf16[2,256,256]{2,1,0:T(8,128)(2,1)S(1)}) fusion(f32[2,48,256]{2,1,0:T(8,128)S(1)} %copy-done.102, f32[2,256,256]{2,1,0:T(8,128)S(1)} %copy-done.67, pred[256,256]{1,0:T(8,128)(4,1)S(1)} %copy-done.105, f32[2,256,48,64]{1,0,3,2:T(2,128)} %reshape.2016, ...), kind=kOutput, calls=%fused_computation.28 | convolution fusion | flops 875905024 | bytes 13828096 | tf_op jit(solution)/shard_map/transpose(jvp(bcgrqs,bcsgrp->bcqgrp))/dot_general | solution.py:33
  641.0 14.6 multiply_reduce_fusion.2
  655.6 20.3 %fusion.78 = (bf16[3328]{0:T(1024)(128)(2,1)}, bf16[3328]{0:T(1024)(128)(2,1)}, bf16[3328]{0:T(1024)(128)(2,1)}, bf16[3328]{0:T(1024)(128)(2,1)}, bf16[3328]{0:T(1024)(128)(2,1)}, /*index=5*/f32[1,512,3328]{1,2,0:T(8,128)}) fusion(bf16[1,512,3328]{1,2,0:T(8,128)(2,1)} %copy-done.6, bf16[1,512,6448]{1,2,0:T(8,128)(2,1)} %copy-done.7, ...), kind=kLoop, calls=%fused_computation.108 | loop fusion | flops 40877824 | bytes 27296256 | tf_op jit(solution)/shard_map/transpose(jvp())/reduce_sum | solution.py:56
  688.5 19.3 %fusion.171 = (bf16[1536]{0:T(1024)(128)(2,1)}, f32[512]{0:T(512)S(1)}, bf16[512,1536]{1,0:T(8,128)(2,1)}) fusion(bf16[1,512,1536]{2,1,0:T(8,128)(2,1)} %copy-done.35, f32[512]{0:T(512)S(1)} %copy-done.145, f32[1536]{0:T(1024)S(1)} %copy-done.118, bf16[1,1536,6448]{1,2,0:T(8,128)(2,1)} %all-gather.27.cloned.1.call-done, ...), kind=kOutput, calls=%fused_computation.265 | convolution fusion | flops 10168711168 | bytes 29570048 | tf_op jit(solution)/shard_map/blk,dk->bld/dot_general | solution.py:85
  722.1 24.9 %multiply_convert_fusion = bf16[1536,6448]{0,1:T(8,128)(2,1)} fusion(bf16[1,512,3328]{1,2,0:T(8,128)(2,1)S(1)} %copy-done.27, bf16[1,512,48]{1,2,0:T(8,128)(2,1)S(1)} %get-tuple-element.96, bf16[1,512,3072]{1,2,0:T(8,128)(2,1)} %get-tuple-element.117, bf16[1,512,1536]{2,1,0:T(8,128)(2,1)} %copy-done.35, f32[1536]{0:T(1024)S(1)} %copy-done.118, ...), kind=kOutput, calls=%fused_computation | convolution fusion | flops 10184589312 | bytes 27992064 | tf_op jit(solution)/shard_map/bld,blk->dk/dot_general | solution.py:84
  747.0 24.8 %copy.744 = bf16[1536,6448]{1,0:T(8,128)(2,1)} copy(bf16[1536,6448]{0,1:T(8,128)(2,1)} %multiply_convert_fusion) | data formatting | bytes 39616512
  780.5 11.3 fusion.118
  825.5 14.3 fusion.117
  856.6 11.3 copy.671
  898.9 18.4 %fusion.23 = (f32[2,48,256]{2,1,0:T(8,128)S(1)}, f32[2,48,256]{2,1,0:T(8,128)S(1)}, bf16[2,256,256]{2,1,0:T(8,128)(2,1)S(1)}) fusion(f32[2,48,256]{2,1,0:T(8,128)} %copy-done.99, f32[2,256,256]{2,1,0:T(8,128)} %copy-done.64, pred[256,256]{1,0:T(8,128)(4,1)} %copy-done.103, f32[2,256,48,64]{1,0,3,2:T(2,128)} %reshape.2001, f32[2,256,48]{1,2,0:T(8,128)S(1)} %copy-done.32, ...), kind=kOutput, calls=%fused_computation.30 | convolution fusion | flops 875905024 | bytes 13828096 | tf_op jit(solution)/shard_map/transpose(jvp(bcgrqs,bcsgrp->bcqgrp))/dot_general | solution.py:33
  941.9 14.1 multiply_reduce_fusion.3
  956.1 19.8 %fusion.70 = (bf16[3328]{0:T(1024)(128)(2,1)S(1)}, bf16[3328]{0:T(1024)(128)(2,1)S(1)}, bf16[3328]{0:T(1024)(128)(2,1)S(1)}, bf16[3328]{0:T(1024)(128)(2,1)S(1)}...) fusion(bf16[1,512,3328]{1,2,0:T(8,128)(2,1)} %copy-done.5, bf16[1,512,6448]{1,2,0:T(8,128)(2,1)} %copy-done.4, ...), kind=kLoop, calls=%fused_computation.100 | loop fusion | flops 40877824 | bytes 27296256 | tf_op jit(solution)/shard_map/transpose(jvp())/reduce_sum | solution.py:56
  989.1 24.1 %multiply_convert_fusion.1 = bf16[1536,6448]{0,1:T(8,128)(2,1)} fusion(bf16[1,512,3328]{1,2,0:T(8,128)(2,1)S(1)} %pad_add_fusion.2, bf16[1,512,48]{1,2,0:T(8,128)(2,1)S(1)} %get-tuple-element.94, bf16[1,512,3072]{1,2,0:T(8,128)(2,1)S(1)} %copy-done.28, bf16[1,512,1536]{2,1,0:T(8,128)(2,1)S(1)} %copy-done.18, f32[1536]{0:T(1024)S(1)} %copy-done.116, ...), kind=kOutput, calls=%fused_computation.1 | convolution fusion | flops 10184589312 | bytes 27992064 | tf_op jit(solution)/shard_map/bld,blk->dk/dot_general | solution.py:84
  1013.2 24.3 %copy.742 = bf16[1536,6448]{1,0:T(8,128)(2,1)} copy(bf16[1536,6448]{0,1:T(8,128)(2,1)} %multiply_convert_fusion.1) | data formatting | bytes 39616512
  1068.9 110.4 %reduce-scatter.19.cloned.1.call-done = bf16[384,6448]{1,0:T(8,128)(2,1)} async-done(((bf16[1536,6448]{1,0:T(8,128)(2,1)}), bf16[384,6448]{1,0:T(8,128)(2,1)}) %reduce-scatter.19.cloned.1.call-update) | async-done | bytes 4952080
  1196.5 18.2 %fusion.173 = (bf16[1536]{0:T(1024)(128)(2,1)S(1)}, f32[512]{0:T(512)S(1)}, bf16[512,1536]{1,0:T(8,128)(2,1)}) fusion(bf16[1,512,1536]{2,1,0:T(8,128)(2,1)S(1)} %copy-done.18, f32[512]{0:T(512)S(1)} %copy-done.143, f32[1536]{0:T(1024)S(1)} %copy-done.116, bf16[1,1536,6448]{1,2,0:T(8,128)(2,1)} %all-gather.23.cloned.1.call-done, ...), kind=kOutput, calls=%fused_computation.267 | convolution fusion | flops 10168711168 | bytes 29570048 | tf_op jit(solution)/shard_map/blk,dk->bld/dot_general | solution.py:85
  1214.9 11.5 all-reduce.58
  1237.1 11.0 fusion.215
  1250.3 19.6 %all-reduce.56 = (f32[1,384]{1,0:T(1,128)S(1)}, f32[1,384]{1,0:T(1,128)S(1)}, f32[1,4,832]{2,1,0:T(4,128)S(1)}, f32[1,4,832]{2,1,0:T(4,128)S(1)}, f32[1,832]{1,0...) all-reduce(f32[1,384]{1,0:T(1,128)S(1)} %stack.82, ...), channel_id=1, replica_groups=mesh['dp'=4,'fsdp'=4] {'dp'}, use_global_device_ids=true, to_apply=%region_43.45 | all-reduce | flops 10696 | bytes 85568 | tf_op jit(solution)/shard_map/psum | solution.py:113
  1274.0 457.5 %all-reduce.62.cloned.1.call-done = (f32[1,384,6448]{1,2,0:T(8,128)}, f32[1,384,6448]{1,2,0:T(8,128)}, f32[1,768,1536]{2,1,0:T(8,128)}, f32[1,768,1536]{2,1,0:T(8,128)}) async-done(((f32[1,384,6448]{1,2,0:T(8,128)}, f32[1,384,6448]{1,2,0:T(8,128)}, f32[1,768,1536]{2,1,0:T(8,128)}, f32[1,768,1536]{2,1,0:T(8,128)}), (f32[1,384,6448]{1,2,0:T(8,128)}, f32[1,384,6448]{1,2,0:T(8,128)}, f32[1,768,1536]{2,1,0:T(8,128)}, ...) | async-done | bytes 29245456 | tf_op jit(solution)/shard_map/psum | solution.py:113
  1731.5 17.1 pad_maximum_fusion
  (732 shorter events, 548.9 us)
Async XLA Ops:
  7.2 254.5 %all-gather.23.cloned.1.call-start = ((), (), s32[]{:S(2)}) async-start(), calls=%async_computation.8 | async-start | bytes 24760320 | tf_op jit(solution)/shard_map/all_gather | solution.py:101
  16.0 336.7 %all-gather.25.cloned.1.call-start = ((), (), s32[]{:S(2)}) async-start(), calls=%async_computation.9 | async-start | bytes 11796480 | tf_op jit(solution)/shard_map/all_gather | solution.py:101
  20.9 344.0 %all-gather.27.cloned.1.call-start = ((), (), s32[]{:S(2)}) async-start(), calls=%async_computation.10 | async-start | bytes 24760320 | tf_op jit(solution)/shard_map/all_gather | solution.py:101
  21.6 444.6 %all-gather.29.cloned.1.call-start = ((), (), s32[]{:S(2)}) async-start(), calls=%async_computation.11 | async-start | bytes 11796480 | tf_op jit(solution)/shard_map/all_gather | solution.py:101
  21.7 118.6 %copy-start.172 = (f32[2,12]{1,0:T(2,128)S(1)}, f32[2,12]{1,0:T(2,128)}, u32[]{:S(2)}) copy-start(f32[2,12]{1,0:T(2,128)} %param.20) | copy-start | bytes 292
  21.8 126.3 %copy-start.140 = (bf16[2,768]{1,0:T(2,128)(2,1)S(1)}, bf16[2,768]{1,0:T(2,128)(2,1)}, u32[]{:S(2)}) copy-start(bf16[2,768]{1,0:T(2,128)(2,1)} %param.21) | copy-start | bytes 9220
  22.2 1019.0 %reduce-scatter.17.cloned.1.call-start = ((), (), s32[]{:S(2)}) async-start(), calls=%async_computation.7 | async-start | bytes 11796480 | tf_op jit(solution)/shard_map/reduce_scatter | solution.py:112
  22.3 286.6 %copy-start.173 = (pred[2,2]{1,0:T(4,128)(4,1)}, pred[2,2]{1,0:T(4,128)(4,1)S(1)}, u32[]{:S(2)}) copy-start(pred[2,2]{1,0:T(4,128)(4,1)S(1)} %iota_compare_fusion.1) | copy-start | bytes 16
  22.4 290.4 %copy-start.103 = (pred[256,256]{1,0:T(8,128)(4,1)}, pred[256,256]{1,0:T(8,128)(4,1)S(1)}, u32[]{:S(2)}) copy-start(pred[256,256]{1,0:T(8,128)(4,1)S(1)} %iota_compare_fusion) | copy-start | bytes 196612
  28.8 232.9 %copy-start.115 = (f32[1536]{0:T(1024)}, f32[1536]{0:T(1024)S(1)}, u32[]{:S(2)}) copy-start(f32[1536]{0:T(1024)S(1)} %convert_reduce_fusion.1) | copy-start | bytes 18436
  29.2 232.5 %copy-start.142 = (f32[512]{0:T(512)}, f32[512]{0:T(512)S(1)}, u32[]{:S(2)}) copy-start(f32[512]{0:T(512)S(1)} %fusion.388) | copy-start | bytes 6148
  124.0 153.4 %copy-start.77 = (f32[3328]{0:T(1024)}, f32[3328]{0:T(1024)S(1)}, u32[]{:S(2)}) copy-start(f32[3328]{0:T(1024)S(1)} %get-tuple-element.45) | copy-start | bytes 39940
  124.0 153.4 %copy-start.79 = (f32[3328]{0:T(1024)}, f32[3328]{0:T(1024)S(1)}, u32[]{:S(2)}) copy-start(f32[3328]{0:T(1024)S(1)} %get-tuple-element.46) | copy-start | bytes 39940
  124.0 153.4 %copy-start.81 = (f32[3328]{0:T(1024)}, f32[3328]{0:T(1024)S(1)}, u32[]{:S(2)}) copy-start(f32[3328]{0:T(1024)S(1)} %get-tuple-element.47) | copy-start | bytes 39940
  124.0 153.4 %copy-start.83 = (f32[3328]{0:T(1024)}, f32[3328]{0:T(1024)S(1)}, u32[]{:S(2)}) copy-start(f32[3328]{0:T(1024)S(1)} %get-tuple-element.48) | copy-start | bytes 39940
  147.4 129.7 %copy-start.161 = (f32[48]{0:T(128)}, f32[48]{0:T(128)S(1)}, u32[]{:S(2)}) copy-start(f32[48]{0:T(128)S(1)} %get-tuple-element.66) | copy-start | bytes 580
  147.4 129.7 %copy-start.166 = (f32[48]{0:T(128)}, f32[48]{0:T(128)S(1)}, u32[]{:S(2)}) copy-start(f32[48]{0:T(128)S(1)} %get-tuple-element.61) | copy-start | bytes 580
  147.4 129.7 %copy-start.168 = (f32[48]{0:T(128)}, f32[48]{0:T(128)S(1)}, u32[]{:S(2)}) copy-start(f32[48]{0:T(128)S(1)} %get-tuple-element.64) | copy-start | bytes 580
  147.4 143.9 %copy-start.151 = (f32[48]{0:T(128)}, f32[48]{0:T(128)S(1)}, u32[]{:S(2)}) copy-start(f32[48]{0:T(128)S(1)} %get-tuple-element.62) | copy-start | bytes 580
  147.4 143.9 %copy-start.153 = (f32[48]{0:T(128)}, f32[48]{0:T(128)S(1)}, u32[]{:S(2)}) copy-start(f32[48]{0:T(128)S(1)} %exponential_negate_fusion.1) | copy-start | bytes 580
  148.0 195.0 %copy-start.74 = (f32[3072]{0:T(1024)}, f32[3072]{0:T(1024)S(1)}, u32[]{:S(2)}) copy-start(f32[3072]{0:T(1024)S(1)} %mul.1214) | copy-start | bytes 36868
  153.4 199.8 %copy-start.94 = (f32[1,3072]{1,0:T(1,128)}, f32[1,3072]{1,0:T(1,128)S(1)}, u32[]{:S(2)}) copy-start(f32[1,3072]{1,0:T(1,128)S(1)} %convert_element_type.633) | copy-start | bytes 36868
  259.8 130.8 %copy-start.85 = (f32[3328]{0:T(1024)}, f32[3328]{0:T(1024)S(1)}, u32[]{:S(2)}) copy-start(f32[3328]{0:T(1024)S(1)} %get-tuple-element.41) | copy-start | bytes 39940
  259.8 130.8 %copy-start.87 = (f32[3328]{0:T(1024)}, f32[3328]{0:T(1024)S(1)}, u32[]{:S(2)}) copy-start(f32[3328]{0:T(1024)S(1)} %get-tuple-element.42) | copy-start | bytes 39940
  259.8 130.8 %copy-start.89 = (f32[3328]{0:T(1024)}, f32[3328]{0:T(1024)S(1)}, u32[]{:S(2)}) copy-start(f32[3328]{0:T(1024)S(1)} %get-tuple-element.43) | copy-start | bytes 39940
  483.5 157.4 %copy-start.129 = (f32[512]{0:T(512)}, f32[512]{0:T(512)S(1)}, u32[]{:S(2)}) copy-start(f32[512]{0:T(512)S(1)} %get-tuple-element.159) | copy-start | bytes 6148
  539.1 507.8 %reduce-scatter.15.cloned.1.call-start = ((), (), s32[]{:S(2)}) async-start(), calls=%async_computation.6 | async-start | bytes 11796480 | tf_op jit(solution)/shard_map/reduce_scatter | solution.py:112
  720.2 333.0 %reduce-scatter.21.cloned.1.call-start = ((), (), s32[]{:S(2)}) async-start(), calls=%async_computation.13 | async-start | bytes 25067520
  771.8 407.5 %reduce-scatter.19.cloned.1.call-start = ((), (), s32[]{:S(2)}) async-start(), calls=%async_computation.12 | async-start | bytes 25067520
  1037.5 210.6 %reduce-scatter.25.cloned.1.call-start = ((), (), s32[]{:S(2)}) async-start(), calls=%async_computation.15 | async-start | bytes 1064960
  1039.7 209.4 %reduce-scatter.23.cloned.1.call-start = ((), (), s32[]{:S(2)}) async-start(), calls=%async_computation.14 | async-start | bytes 1064960
  1041.2 690.4 %all-reduce.62.cloned.1.call-start = ((), (), s32[]{:S(2)}) async-start(), calls=%async_computation.16 | async-start | bytes 58490880 | tf_op jit(solution)/shard_map/psum | solution.py:113
  (176 other events, 2141.3 us)
Sparse Core Ops, SparseCore 0:
  16.2 135.2 all-gather.22
  153.0 71.4 all-gather.24
  226.7 122.9 all-gather.26
  351.1 62.3 all-gather.28
  539.2 74.1 reduce-scatter.16
  720.3 74.1 reduce-scatter.14
  797.1 141.2 reduce-scatter.20
  1037.6 141.6 reduce-scatter.18
  1181.8 19.8 reduce-scatter.24
  1204.1 20.3 reduce-scatter.22
  1229.2 502.2 all-reduce.61
where the time goes:
time: 1770 us; the launch traced here: 1760 us
  waiting for transfers between devices  569 us (32%)
  other arithmetic  406 us (23%)
  local copies, waits for them, and re-layouts  320 us (18%)
  matrix products  317 us (18%)
  blocking collectives  126 us (7%)
  between operations  21.1 us (1%)
    psum x1, waiting for transfers between devices, reduce_layer(): out_pieces.append(lax.psum(summed.astype(jnp.float32), 'dp'))  458 us
    convert_element_type x2, other arithmetic, mixer_core(): conv_w[tap].astype(jnp.float32)  141 us
    unnamed x427, local copies, waits for them, and re-layouts  118 us
    unnamed x15, waiting for transfers between devices  112 us
    dot_general x6, matrix products, ssd_chunks(): jnp.einsum('bcgrqs,bcsgrp->bcqgrp', scores[:, :, :, None] * decay_mat, x_...  70.7 us
    all_gather x6, blocking collectives, gather_layer(): lax.all_gather(piece[layer], 'fsdp', axis=axis_id, tiled=True)  69.2 us
    another operation x14, other arithmetic, per_device(): jnp.stack([first, second])  51.9 us
    dot_general x2, matrix products, layer_backward(): jnp.einsum('bld,blk->dk', h_norm, d_proj, preferred_element_type=jnp.floa...  49 us
  transfers between devices with their start and end apart: 11, of which 2 were waited for; matrix products, arithmetic and copies ran while one was open for 51% of the time, Pallas kernels for 0%

commit v1 on v0

v1 whole, which is shorter than its diff:
```python
import jax
import jax.numpy as jnp
from jax import lax
from jax.experimental import pallas as pl
from jax.experimental.pallas import tpu as pltpu
from jax.sharding import PartitionSpec as P


CHUNK = 256
SEQ = 512
LANES = 128
HEAD = 64
D_MODEL = 1536
D_INNER = 3072
N_HEADS = 48
CONV_DIM = 3328
PROJ = 6448
PROJ_PAD = 6528
N_PAIRS = N_HEADS // 2
NORM_EPS = 1e-5
F32 = jnp.float32
BF16 = jnp.bfloat16
NT = (((1,), (1,)), ((), ()))
TN = (((0,), (0,)), ((), ()))


def _dot(a, b):
    return jnp.dot(a, b, preferred_element_type=F32)


def _dot_dims(a, b, dims):
    return lax.dot_general(a, b, dims, preferred_element_type=F32)


def _iota(shape, dim):
    return lax.broadcasted_iota(jnp.int32, shape, dim)


def _later(x, k):
    if k == 0:
        return x
    return jnp.where(_iota(x.shape, 0) >= k, pltpu.roll(x, k, 0), 0.0)


def _sooner(x, k):
    if k == 0:
        return x
    n = x.shape[0]
    return jnp.where(_iota(x.shape, 0) < n - k, pltpu.roll(x, n - k, 0), 0.0)


def _conv(x_in, taps):
    out = taps[4:5] + x_in * taps[3:4]
    for k in range(3):
        out += _later(x_in, 3 - k) * taps[k:k + 1]
    return out


def _conv_back(d_out, x_in, taps):
    d_in = d_out * taps[3:4]
    for k in range(3):
        d_in += _sooner(d_out, 3 - k) * taps[k:k + 1]
    rows = [jnp.sum(d_out * _later(x_in, 3 - k), axis=0, keepdims=True) for k in range(4)]
    rows.append(jnp.sum(d_out, axis=0, keepdims=True))
    return d_in, rows


def _sigmoid(x):
    return 1.0 / (1.0 + jnp.exp(-x))


def _silu_grad(x, sig):
    return sig * (1.0 + x * (1.0 - sig))


def _pair(a, b):
    shape = (max(a.shape[0], b.shape[0]), LANES)
    return jnp.where(_iota(shape, 1) < HEAD, a, b)


def _scores(b_ref, c_ref, tb_ref, tc_ref, b_sc, c_sc, g_sc):
    for ref, taps, dst in ((b_ref, tb_ref, b_sc), (c_ref, tc_ref, c_sc)):
        pre = _conv(ref[...].astype(F32), taps[...])
        dst[...] = (pre * _sigmoid(pre)).astype(BF16)
    causal = _iota((CHUNK, CHUNK), 0) >= _iota((CHUNK, CHUNK), 1)
    for c in range(2):
        sl = pl.ds(c * CHUNK, CHUNK)
        g_sc[c] = jnp.where(causal, _dot_dims(c_sc[sl, :], b_sc[sl, :], NT), 0.0)


def _decay(rows, cols, c, h):
    lo, hi = c * CHUNK, (c + 1) * CHUNK
    return jnp.exp(jnp.minimum(cols[lo:hi, 2 + h:3 + h] - rows[2 + h:3 + h, lo:hi], 0.0))


def _state(x_dt, rows, cols, b_sc):
    end = _pair(rows[2:3, CHUNK - 1:CHUNK], rows[3:4, CHUNK - 1:CHUNK])
    weight = jnp.exp(jnp.minimum(end - _pair(cols[:CHUNK, 2:3], cols[:CHUNK, 3:4]), 0.0))
    x_end = (x_dt[:CHUNK] * weight).astype(BF16)
    state = _dot_dims(x_end, b_sc[pl.ds(0, CHUNK), :], TN).astype(BF16)
    return state, x_end, weight


def fwd_kernel(rows_ref, x_ref, z_ref, b_ref, c_ref, tx_ref, tb_ref, tc_ref, par_ref,
               y_ref, n_ref, r_ref, b_sc, c_sc, g_sc, v_sc, acc):
    j = pl.program_id(0)

    @pl.when(j == 0)
    def _():
        _scores(b_ref, c_ref, tb_ref, tc_ref, b_sc, c_sc, g_sc)
        acc[...] = jnp.zeros_like(acc)

    rows = rows_ref[0]
    cols = rows.T
    pre = _conv(x_ref[...].astype(F32), tx_ref[...])
    x = pre * _sigmoid(pre)
    x_dt = x * _pair(cols[:, 0:1], cols[:, 1:2])
    x_b = x_dt.astype(BF16)
    y_parts = []
    for c in range(2):
        lo, hi = c * CHUNK, (c + 1) * CHUNK
        heads = [_dot((g_sc[c] * _decay(rows, cols, c, h)).astype(BF16), x_b[lo:hi]) for h in range(2)]
        y_parts.append(_pair(heads[0], heads[1]))
    state, _, _ = _state(x_dt, rows, cols, b_sc)
    from_start = jnp.exp(_pair(cols[CHUNK:, 2:3], cols[CHUNK:, 3:4]))
    y_parts[1] += from_start * _dot_dims(c_sc[pl.ds(CHUNK, CHUNK), :], state, NT)
    lane0 = pl.multiple_of(j * LANES, LANES)
    y = jnp.concatenate(y_parts, axis=0) + par_ref[1:2, pl.ds(lane0, LANES)] * x
    y_ref[...] = y
    z = z_ref[...].astype(F32)
    v = y * (z * _sigmoid(z))
    v_sc[j] = v
    acc[...] += v * v

    @pl.when(j == N_PAIRS - 1)
    def _():
        r = lax.rsqrt(jnp.sum(acc[...], axis=1, keepdims=True) / D_INNER + NORM_EPS)
        r_full = jnp.broadcast_to(r, (SEQ, LANES))
        r_ref[...] = r_full

        @pl.loop(0, N_PAIRS)
        def _(i):
            at = pl.ds(pl.multiple_of(i * LANES, LANES), LANES)
            n_ref[:, at] = (v_sc[i] * r_full * par_ref[0:1, at]).astype(BF16)


def bwd_kernel(rows_ref, x_ref, z_ref, b_ref, c_ref, y_ref, dn_ref, r_ref, tx_ref, tb_ref, tc_ref, par_ref,
               dp_ref, drows_ref, gch_ref, gbc_ref, b_sc, c_sc, g_sc, dg_sc, dc_sc, db_sc, acc):
    phase, j = pl.program_id(0), pl.program_id(1)
    gate = par_ref[0:1]
    skip = par_ref[1:2]
    z = z_ref[...].astype(F32)
    sig_z = _sigmoid(z)
    act_z = z * sig_z
    y = y_ref[...]
    v = y * act_z
    d_n = dn_ref[...].astype(F32)
    d_vn = d_n * gate

    @pl.when(phase == 0)
    def _():
        @pl.when(j == 0)
        def _():
            acc[...] = jnp.zeros_like(acc)

        acc[...] += d_vn * v

    @pl.when(phase == 1)
    def _():
        @pl.when(j == 0)
        def _():
            total = jnp.sum(acc[...], axis=1, keepdims=True) / D_INNER
            acc[...] = jnp.broadcast_to(total, (SEQ, LANES))
            _scores(b_ref, c_ref, tb_ref, tc_ref, b_sc, c_sc, g_sc)
            dg_sc[...] = jnp.zeros_like(dg_sc)
            dc_sc[...] = jnp.zeros_like(dc_sc)
            db_sc[...] = jnp.zeros_like(db_sc)

        r = r_ref[...]
        d_v = r * d_vn - v * (r * r * r) * acc[...]
        g_gate = jnp.sum(d_n * v * r, axis=0, keepdims=True)
        lane0 = pl.multiple_of(j * LANES, LANES)
        dp_ref[:, pl.ds(lane0, LANES)] = (d_v * y * _silu_grad(z, sig_z)).astype(BF16)
        d_y = d_v * act_z

        rows = rows_ref[0]
        cols = rows.T
        x_in = x_ref[...].astype(F32)
        pre = _conv(x_in, tx_ref[...])
        sig_x = _sigmoid(pre)
        x = pre * sig_x
        dt = _pair(cols[:, 0:1], cols[:, 1:2])
        x_dt = x * dt
        x_b = x_dt.astype(BF16)
        x_r = x_b.astype(F32)
        g_skip = jnp.sum(d_y * x, axis=0, keepdims=True)
        dy_b = d_y.astype(BF16)
        dy_r = dy_b.astype(F32)
        dy_t = dy_r.T.astype(BF16)
        first = _iota((CHUNK, LANES), 1) < HEAD
        dx_parts = []
        for c in range(2):
            lo, hi = c * CHUNK, (c + 1) * CHUNK
            halves = []
            for h in range(2):
                decay = _decay(rows, cols, c, h)
                mixed = (g_sc[c] * decay).astype(BF16)
                own = first if h == 0 else jnp.logical_not(first)
                dy_h = jnp.where(own, dy_r[lo:hi], 0.0).astype(BF16)
                dg_sc[c] += _dot_dims(dy_h, x_b[lo:hi], NT) * decay
                halves.append(_dot(dy_t[h * HEAD:(h + 1) * HEAD, lo:hi], mixed))
            dx_parts.append(jnp.concatenate(halves, axis=0).T)
        state, x_end, weight = _state(x_dt, rows, cols, b_sc)
        dy_off = dy_r[CHUNK:] * jnp.exp(_pair(cols[CHUNK:, 2:3], cols[CHUNK:, 3:4]))
        dc_sc[...] += _dot(dy_off.astype(BF16), state)
        d_state = _dot(dy_off.T.astype(BF16), c_sc[pl.ds(CHUNK, CHUNK), :]).astype(BF16)
        db_sc[...] += _dot(x_end, d_state)
        dx_state = weight * _dot_dims(b_sc[pl.ds(0, CHUNK), :], d_state, NT)
        dx_parts[0] += dx_state
        d_xdt = jnp.concatenate(dx_parts, axis=0)
        end_sum = jnp.sum(x_r[:CHUNK] * dx_state, axis=0, keepdims=True)
        d_cum = dy_r * (y - skip * x) - x_r * d_xdt
        d_cum += jnp.where(_iota((SEQ, LANES), 0) == CHUNK - 1, end_sum, 0.0)
        dt_t = (d_xdt * x).T
        cum_t = d_cum.T
        drows_ref[0] = jnp.concatenate(
            [jnp.sum(part[h * HEAD:(h + 1) * HEAD], axis=0, keepdims=True) for part in (dt_t, cum_t) for h in range(2)]
            + [jnp.zeros((4, SEQ), F32)], axis=0)
        d_pre = (d_xdt * dt + skip * d_y) * _silu_grad(pre, sig_x)
        d_in, g_rows = _conv_back(d_pre, x_in, tx_ref[...])
        dp_ref[:, pl.ds(pl.multiple_of(D_INNER + lane0, LANES), LANES)] = d_in.astype(BF16)
        gch_ref[...] = jnp.concatenate(g_rows + [g_gate, g_skip, jnp.zeros((1, LANES), F32)], axis=0)

        @pl.when(j == N_PAIRS - 1)
        def _():
            causal = _iota((CHUNK, CHUNK), 0) >= _iota((CHUNK, CHUNK), 1)
            d_b, d_c = [], []
            for c in range(2):
                sl = pl.ds(c * CHUNK, CHUNK)
                d_g = jnp.where(causal, dg_sc[c], 0.0)
                d_c.append(_dot(d_g.astype(BF16), b_sc[sl, :]))
                d_b.append(_dot(d_g.T.astype(BF16), c_sc[sl, :]))
            d_c[1] += dc_sc[...]
            d_b[0] += db_sc[...]
            for i, (parts, ref, taps) in enumerate(((d_b, b_ref, tb_ref), (d_c, c_ref, tc_ref))):
                val = ref[...].astype(F32)
                pre_i = _conv(val, taps[...])
                d_pre_i = jnp.concatenate(parts, axis=0) * _silu_grad(pre_i, _sigmoid(pre_i))
                d_val, g_val = _conv_back(d_pre_i, val, taps[...])
                dp_ref[:, pl.ds(2 * D_INNER + i * LANES, LANES)] = d_val.astype(BF16)
                gbc_ref[:, pl.ds(i * LANES, LANES)] = jnp.concatenate(g_val + [jnp.zeros((3, LANES), F32)], axis=0)
            dp_ref[:, pl.ds(2 * D_INNER + 2 * LANES, LANES)] = jnp.zeros((SEQ, LANES), BF16)


def _col(block):
    return pl.BlockSpec((SEQ, LANES), lambda j: (0, block(j)))


def part_rows(rows):
    return -(-rows // 64) * 16


def mixer_fwd(proj, rows, taps, par):
    taps_at = lambda block: pl.BlockSpec((8, LANES), lambda j: (0, block(j)))
    return pl.pallas_call(
        fwd_kernel,
        grid=(N_PAIRS,),
        in_specs=[
            pl.BlockSpec((1, 8, SEQ), lambda j: (j, 0, 0)),
            _col(lambda j: N_PAIRS + j), _col(lambda j: j), _col(lambda j: 2 * N_PAIRS), _col(lambda j: 2 * N_PAIRS + 1),
            taps_at(lambda j: j), taps_at(lambda j: N_PAIRS), taps_at(lambda j: N_PAIRS + 1),
            pl.BlockSpec((8, D_INNER), lambda j: (0, 0)),
        ],
        out_specs=[_col(lambda j: j), pl.BlockSpec((SEQ, D_INNER), lambda j: (0, 0)), pl.BlockSpec((SEQ, LANES), lambda j: (0, 0))],
        out_shape=[
            jax.ShapeDtypeStruct((SEQ, D_INNER), F32),
            jax.ShapeDtypeStruct((SEQ, D_INNER), BF16),
            jax.ShapeDtypeStruct((SEQ, LANES), F32),
        ],
        scratch_shapes=[
            pltpu.VMEM((SEQ, LANES), BF16), pltpu.VMEM((SEQ, LANES), BF16), pltpu.VMEM((2, CHUNK, CHUNK), F32),
            pltpu.VMEM((N_PAIRS, SEQ, LANES), F32), pltpu.VMEM((SEQ, LANES), F32),
        ],
        compiler_params=pltpu.CompilerParams(dimension_semantics=("arbitrary",), vmem_limit_bytes=40 * 2 ** 20),
        cost_estimate=pl.CostEstimate(flops=8 * 10 ** 9, bytes_accessed=16 * 10 ** 6, transcendentals=10 ** 7),
        name="mixer_fwd",
    )(rows, proj, proj, proj, proj, taps, taps, taps, par)


def mixer_bwd(proj, rows, taps, par, y, d_n, r):
    col = lambda block: pl.BlockSpec((SEQ, LANES), lambda f, j: (0, block(f, j)))
    taps_at = lambda block: pl.BlockSpec((8, LANES), lambda f, j: (0, block(f, j)))
    return pl.pallas_call(
        bwd_kernel,
        grid=(2, N_PAIRS),
        in_specs=[
            pl.BlockSpec((1, 8, SEQ), lambda f, j: (f * j, 0, 0)),
            col(lambda f, j: N_PAIRS + f * j), col(lambda f, j: j), col(lambda f, j: 2 * N_PAIRS), col(lambda f, j: 2 * N_PAIRS + 1),
            col(lambda f, j: j), col(lambda f, j: j), col(lambda f, j: 0),
            taps_at(lambda f, j: f * j), taps_at(lambda f, j: N_PAIRS), taps_at(lambda f, j: N_PAIRS + 1), taps_at(lambda f, j: j),
        ],
        out_specs=[
            pl.BlockSpec((SEQ, PROJ_PAD), lambda f, j: (0, 0)),
            pl.BlockSpec((1, 8, SEQ), lambda f, j: (f * j, 0, 0)),
            taps_at(lambda f, j: f * j),
            pl.BlockSpec((8, 2 * LANES), lambda f, j: (0, 0)),
        ],
        out_shape=[
            jax.ShapeDtypeStruct((SEQ, PROJ_PAD), BF16),
            jax.ShapeDtypeStruct((N_PAIRS, 8, SEQ), F32),
            jax.ShapeDtypeStruct((8, D_INNER), F32),
            jax.ShapeDtypeStruct((8, 2 * LANES), F32),
        ],
        scratch_shapes=[
            pltpu.VMEM((SEQ, LANES), BF16), pltpu.VMEM((SEQ, LANES), BF16), pltpu.VMEM((2, CHUNK, CHUNK), F32),
            pltpu.VMEM((2, CHUNK, CHUNK), F32), pltpu.VMEM((CHUNK, LANES), F32), pltpu.VMEM((CHUNK, LANES), F32),
            pltpu.VMEM((SEQ, LANES), F32),
        ],
        compiler_params=pltpu.CompilerParams(dimension_semantics=("arbitrary", "arbitrary"), vmem_limit_bytes=40 * 2 ** 20),
        cost_estimate=pl.CostEstimate(flops=16 * 10 ** 9, bytes_accessed=40 * 10 ** 6, transcendentals=10 ** 7),
        name="mixer_bwd",
    )(rows, proj, proj, proj, proj, y, d_n, r, taps, taps, taps, par)


def pre_norm(u_rows, norm_w):
    rows_f = u_rows.astype(F32)
    inv_rms = lax.rsqrt(jnp.mean(jnp.square(rows_f), axis=-1, keepdims=True) + NORM_EPS)
    return (rows_f * inv_rms * norm_w.astype(F32)).astype(BF16)


def head_rows(dt_raw, dt_bias, a_log):
    dt = jax.nn.softplus(dt_raw.astype(F32) + dt_bias).T
    a = dt * -jnp.exp(a_log)[:, None]
    upto = (jnp.arange(CHUNK)[:, None] <= jnp.arange(CHUNK)[None, :]).astype(F32)
    cum = jnp.einsum('hcs,st->hct', a.reshape(N_HEADS, SEQ // CHUNK, CHUNK), upto, precision=lax.Precision.HIGHEST)
    pairs = (N_PAIRS, 2, SEQ)
    return jnp.concatenate([dt.reshape(pairs), cum.reshape(pairs), jnp.zeros((N_PAIRS, 4, SEQ), F32)], axis=1)


def layer_forward(u_rows, small, w_in, w_out):
    norm_w, taps, par, dt_bias, a_log = small
    h_norm, norm_pull = jax.vjp(pre_norm, u_rows, norm_w)
    proj = jnp.dot(h_norm, w_in, preferred_element_type=F32).astype(BF16)
    rows, rows_pull = jax.vjp(head_rows, proj[:, 2 * D_INNER + 2 * LANES:], dt_bias, a_log)
    y, y_norm, r = mixer_fwd(proj, rows, taps, par)
    out = (u_rows.astype(F32) + jnp.dot(y_norm, w_out, preferred_element_type=F32)).astype(BF16)
    return out, (h_norm, norm_pull, proj, rows, rows_pull, y, y_norm, r)


COL_CHUNKS = ((0, 2176), (2176, 4352), (4352, 6528))


def solution(mesh):
    dp_size = mesh.shape['dp']
    fsdp_size = mesh.shape['fsdp']
    act_spec = P(('dp', 'fsdp'), None, None)
    weight_specs = (P(None, 'fsdp'), P(None, 'fsdp', None), P(None, None, 'fsdp'), P(None, 'fsdp'), P(None, 'fsdp'), P(None, 'fsdp'), P(None, 'fsdp'), P(None, 'fsdp'), P(None, 'fsdp', None))

    def per_device(u_loc, g_loc, norm_w, w_in, conv_w, conv_b, dt_bias, a_log, d_skip, gate_w, w_out):
        batch_tot = dp_size * fsdp_size
        me_dp = lax.axis_index('dp')
        me_fsdp = lax.axis_index('fsdp')

        small_pieces = [norm_w, conv_w.reshape(2, -1), conv_b, gate_w, dt_bias, a_log, d_skip]
        widths = [piece.shape[1] for piece in small_pieces]
        packed = jnp.concatenate([piece.astype(F32) for piece in small_pieces], axis=1)
        gathered = lax.all_gather(packed, 'fsdp', axis=0)

        def small_layer(layer):
            vals, at = [], 0
            for width in widths:
                vals.append(gathered[:, layer, at:at + width])
                at += width
            norm, cw, cb, gate, bias, alog, skip = vals
            taps = jnp.concatenate([
                cw.reshape(fsdp_size, 4, -1).transpose(1, 0, 2).reshape(4, CONV_DIM), cb.reshape(1, CONV_DIM),
                jnp.zeros((3, CONV_DIM), F32)], axis=0)
            par = jnp.concatenate([
                gate.reshape(1, D_INNER), jnp.repeat(skip.reshape(N_HEADS), HEAD).reshape(1, D_INNER),
                jnp.zeros((6, D_INNER), F32)], axis=0)
            return norm.reshape(D_MODEL), taps, par, bias.reshape(N_HEADS), alog.reshape(N_HEADS)

        def gather_in_order(pieces):
            full, fulls = None, []
            for piece in pieces:
                if full is not None:
                    piece, full = lax.optimization_barrier((piece, full))
                    fulls.append(full)
                full = lax.all_gather(piece, 'fsdp', axis=0, tiled=True)
            return fulls + [full]

        def partial_grad(left, right):
            return (lax.dot_general(left, right, TN, preferred_element_type=F32) / batch_tot).astype(BF16)

        def spread(part, flip=False, valid=None):
            piece = lax.psum_scatter(part, 'fsdp', scatter_dimension=0, tiled=True)
            piece = piece.T if flip else piece
            rows = piece.shape[0] if valid is None else valid
            size = part_rows(rows)

            def quarter(k):
                return lax.dynamic_slice_in_dim(piece, jnp.minimum((me_dp ^ k) * size, rows - size), size, 0)

            sent = [quarter(k) for k in range(dp_size)]
            terms = sent[:1]
            for k in range(1, dp_size):
                terms.append(lax.ppermute(sent[k], 'dp', [(i, i ^ k) for i in range(dp_size)]))
            terms = [term.astype(F32) for term in terms]
            total = (terms[0] + terms[1]) + (terms[2] + terms[3])
            return [total] + [lax.ppermute(total, 'dp', [(i, i ^ k) for i in range(dp_size)]) for k in range(1, dp_size)]

        def place(buf, layer, parts, first, rows):
            for k, part in enumerate(parts):
                row = first + jnp.minimum((me_dp ^ k) * part.shape[0], rows - part.shape[0])
                buf = lax.dynamic_update_slice(buf, part[None], (layer, row, 0))
            return buf

        def layer_backward(d_out, saved, small, full_in, full_out):
            _, taps, par, _, _ = small
            h_norm, norm_pull, proj, rows, rows_pull, y, y_norm, r = saved
            g_out_part = partial_grad(y_norm, d_out)
            d_out, g_out_part = lax.optimization_barrier((d_out, g_out_part))
            out_parts = spread(g_out_part)
            d_n = lax.dot_general(d_out, full_out, NT, preferred_element_type=F32).astype(BF16)
            d_proj, d_rows, g_ch, g_bc = mixer_bwd(proj, rows, taps, par, y, d_n, r)
            d_raw, g_bias, g_alog = rows_pull(d_rows)
            d_proj = lax.dynamic_update_slice(d_proj, d_raw, (0, 2 * D_INNER + 2 * LANES))
            g_in_parts = [partial_grad(h_norm, d_proj[:, lo:hi]) for lo, hi in COL_CHUNKS]
            d_proj, g_in_parts = lax.optimization_barrier((d_proj, g_in_parts))
            in_parts = [spread(part, flip=True, valid=min(hi, PROJ) - lo) for part, (lo, hi) in zip(g_in_parts, COL_CHUNKS)]
            d_h = lax.dot_general(d_proj[:, :PROJ], full_in, NT, preferred_element_type=F32).astype(BF16)
            d_u_norm, g_norm = norm_pull(d_h)
            d_u = (d_out.astype(F32) + d_u_norm.astype(F32)).astype(BF16)
            g_conv = jnp.concatenate([g_ch[:5], g_bc[:5]], axis=1)
            g_skip = jnp.sum(g_ch[6].reshape(N_HEADS, HEAD), axis=1)
            smalls = [g_norm, g_conv[:4], g_conv[4], g_ch[5], g_bias, g_alog, g_skip]
            return d_u, out_parts, in_parts, smalls

        u_rows, d_out = u_loc[0], g_loc[0]
        small_one, small_two = small_layer(0), small_layer(1)
        in_one, out_one, in_two, out_two = gather_in_order([w_in[0], w_out[0], w_in[1], w_out[1]])
        hidden, saved_one = layer_forward(u_rows, small_one, in_one, out_one)
        out_rows, saved_two = layer_forward(hidden, small_two, in_two, out_two)
        d_hidden, out_parts_two, in_parts_two, smalls_two = layer_backward(d_out, saved_two, small_two, in_two, out_two)
        d_u, out_parts_one, in_parts_one, smalls_one = layer_backward(d_hidden, saved_one, small_one, in_one, out_one)

        g_in = jnp.zeros((2, PROJ, w_in.shape[1]), F32)
        g_out = jnp.zeros((2,) + w_out.shape[1:], F32)
        g_out = place(g_out, 1, out_parts_two, 0, g_out.shape[1])
        for (lo, hi), parts in zip(COL_CHUNKS, in_parts_two):
            g_in = place(g_in, 1, parts, lo, min(hi, PROJ) - lo)
        g_out = place(g_out, 0, out_parts_one, 0, g_out.shape[1])
        for (lo, hi), parts in zip(COL_CHUNKS, in_parts_one):
            g_in = place(g_in, 0, parts, lo, min(hi, PROJ) - lo)

        def small_piece_rows(smalls):
            vals = []
            for idx, grad in enumerate(smalls):
                grad = grad.astype(F32) / batch_tot
                if idx < 4:
                    grad = grad.astype(BF16).astype(F32)
                if idx == 1:
                    grad = grad.reshape(4, fsdp_size, -1).transpose(1, 0, 2)
                vals.append(grad.reshape(fsdp_size, -1))
            return jnp.concatenate(vals, axis=1)

        both = jnp.stack([small_piece_rows(smalls_one), small_piece_rows(smalls_two)], axis=1)
        for axis in ('fsdp', 'dp'):
            for k in (1, 2):
                both = both + lax.ppermute(both, axis, [(i, i ^ k) for i in range(4)])
        summed = lax.dynamic_index_in_dim(both, me_fsdp, 0, keepdims=False)
        outs, at = [], 0
        for width in widths:
            outs.append(summed[:, at:at + width])
            at += width
        g_norm, g_cw, g_cb, g_gate, g_bias, g_alog, g_skip = outs
        return (out_rows[None], d_u[None], g_norm, g_in.swapaxes(1, 2), g_cw.reshape(conv_w.shape), g_cb, g_bias, g_alog, g_skip, g_gate, g_out)

    return jax.shard_map(per_device, mesh=mesh, in_specs=(act_spec, act_spec) + weight_specs, out_specs=(act_spec, act_spec) + weight_specs, check_vma=False)
```

time: 1770 us -> 1410 us (0.80)
  other arithmetic: 406 us -> 32.1 us
  Pallas kernels: 0 us -> 178 us
  matrix products: 317 us -> 191 us
  waiting for transfers between devices: 569 us -> 695 us
  blocking collectives: 126 us -> 5.53 us
  local copies, waits for them, and re-layouts: 320 us -> 215 us
  starting transfers between devices: 0.66 us -> 66 us
    psum x1 -> x0, waiting for transfers between devices: 458 us -> none  [reduce_layer(): out_pieces.append(lax.psum(summed.astype(jnp.float32), 'dp'))]
    all_gather x4, waiting for transfers between devices: 0.05 us -> 310 us  [gather_in_order(): full = lax.all_gather(piece, 'fsdp', axis=0, tiled=True)]
    ppermute x0 -> x52, waiting for transfers between devices: none -> 238 us  [the longest x24 100 us: spread(): lax.ppermute(total, 'dp', [(i, i ^ k) for i in range(dp_size)])]
    pallas_call x0 -> x4, Pallas kernels: none -> 178 us  [the longest x2 126 us: mixer_bwd(): pl.pallas_call(bwd_kernel, grid=(2, N_PAIRS), in_specs=[pl.BlockSpec((1,...]
    convert_element_type x23 -> x5, other arithmetic: 161 us -> 1.02 us  [the longest x1 0.91 us: layer_backward(): d_u = (d_out.astype(F32) + d_u_norm.astype(F32)).astype(BF16)]
    reduce_scatter x2 -> x8, waiting for transfers between devices: 0.02 us -> 144 us  [spread(): piece = lax.psum_scatter(part, 'fsdp', scatter_dimension=0, tiled=True)]
    reduce_sum x17 -> x6, other arithmetic: 141 us -> 4.93 us  [the longest x2 2.4 us: head_rows(): dt = jax.nn.softplus(dt_raw.astype(F32) + dt_bias).T]
    dot_general x42 -> x20, matrix products: 317 us -> 191 us  [the longest x8 64.6 us: partial_grad(): lax.dot_general(left, right, TN, preferred_element_type=F32) / batch_tot]
  transfers between devices with their start and end apart: 11 -> 64, of which waited for: 2 -> 25; matrix products, arithmetic and copies ran while one was open for 51% -> 29% of each run, Pallas kernels for 0% -> 13%
where the time goes in v1:
time: 1410 us; the launch traced here: 1400 us
  waiting for transfers between devices  695 us (49%)
  local copies, waits for them, and re-layouts  215 us (15%)
  matrix products  191 us (14%)
  Pallas kernels  178 us (13%)
  starting transfers between devices  66 us (5%)
  other arithmetic  32.1 us (2%)
  between operations  15.7 us (1%)
    all_gather x4, waiting for transfers between devices, gather_in_order(): full = lax.all_gather(piece, 'fsdp', axis=0, tiled=True)  310 us
    reduce_scatter x8, waiting for transfers between devices, spread(): piece = lax.psum_scatter(part, 'fsdp', scatter_dimension=0, tiled=True)  144 us
    pallas_call x2, Pallas kernels, mixer_bwd(): pl.pallas_call(bwd_kernel, grid=(2, N_PAIRS), in_specs=[pl.BlockSpec((1,...  126 us
    dynamic_update_slice x32, local copies, waits for them, and re-layouts, place(): buf = lax.dynamic_update_slice(buf, part[None], (layer, row, 0))  118 us
    ppermute x24, waiting for transfers between devices, spread(): lax.ppermute(total, 'dp', [(i, i ^ k) for i in range(dp_size)])  100 us
    ppermute x24, waiting for transfers between devices, spread(): lax.ppermute(sent[k], 'dp', [(i, i ^ k) for i in range(dp_size)])  86.4 us
    dot_general x8, matrix products, partial_grad(): lax.dot_general(left, right, TN, preferred_element_type=F32) / batch_tot  64.6 us
    pallas_call x2, Pallas kernels, mixer_fwd(): pl.pallas_call(fwd_kernel, grid=(N_PAIRS,), in_specs=[pl.BlockSpec((1, 8,...  52.3 us
  transfers between devices with their start and end apart: 64, of which 25 were waited for; matrix products, arithmetic and copies ran while one was open for 29% of the time, Pallas kernels for 13%

profile of v1, /device:TPU:0, one launch (start us, length us, event | category | flops | bytes accessed | tf_op | source)
XLA Modules:
  0.0 1398.5 jit_solution(8876909442501133812)
XLA Ops:
  21.0 121.0 %all-gather.14.cloned.1.call-done = bf16[1,1536,6448]{1,2,0:T(8,128)(2,1)} async-done(((bf16[1,384,6448]{1,2,0:T(8,128)(2,1)}), bf16[1,1536,6448]{1,2,0:T(8,128)(2,1)}) %all-gather.14.cloned.1.call-update) | async-done | bytes 19808272 | tf_op jit(solution)/shard_map/all_gather | solution.py:389
  142.0 63.8 %all-gather.8.cloned.1.call-done = bf16[3072,1536]{1,0:T(8,128)(2,1)} async-done(((bf16[768,1536]{1,0:T(8,128)(2,1)}), bf16[3072,1536]{1,0:T(8,128)(2,1)}) %all-gather.8.cloned.1.call-update) | async-done | bytes 9437200 | tf_op jit(solution)/shard_map/all_gather | solution.py:389
  206.0 125.0 %all-gather.10.cloned.1.call-done = bf16[1536,6448]{0,1:T(8,128)(2,1)} async-done(((bf16[384,6448]{0,1:T(8,128)(2,1)}), bf16[1536,6448]{0,1:T(8,128)(2,1)}) %all-gather.10.cloned.1.call-update) | async-done | bytes 19808272 | tf_op jit(solution)/shard_map/all_gather | solution.py:389
  341.0 18.1 %convolution_convert_fusion.1.x_ref.z_ref.b_ref.c_ref = bf16[512,6448]{1,0:T(8,128)(2,1)} fusion(bf16[1536,6448]{0,1:T(8,128)(2,1)} %bitcast.254, bf16[1,512,1536]{2,1,0:T(8,128)(2,1)S(1)} %copy-done.19, f32[1536]{0:T(1024)S(1)} %mul.125, f32[512]{0:T(512)S(1)} %fusion.83), kind=kOutput, calls=%fused_computation.15 | convolution fusion | flops 10148274176 | bytes 27992064 | tf_op jit(solution)/shard_map/dot_general | solution.py:343
  362.1 26.2 %mixer_fwd.2 = (f32[512,3072]{1,0:T(8,128)S(1)}, bf16[512,3072]{1,0:T(8,128)(2,1)S(1)}, f32[512,128]{1,0:T(8,128)S(1)}) custom-call(f32[24,8,512]{2,1,0:T(8,128)S(1)} %maximum_maximum_fusion.rows_ref, bf16[512,6448]{1,0:T(8,128)(2,1)} %convolution_convert_fusion.1.x_ref.z_ref.b_ref.c_ref, ...), custom_call_target="tpu_custom_call" | custom-call | flops 8000000000 | bytes 16000000 | tf_op jit(solution)/shard_map/mixer_fwd/pallas_call | solution.py:265
  388.3 13.3 fusion.22
  401.6 28.4 %convolution_convert_fusion.x_ref.z_ref.b_ref.c_ref = bf16[512,6448]{1,0:T(8,128)(2,1)} fusion(bf16[1536,6448]{0,1:T(8,128)(2,1)} %all-gather.10.cloned.1.call-done, bf16[512,1536]{1,0:T(8,128)(2,1)} %get-tuple-element.157, f32[1536]{0:T(1024)S(1)} %mul.260, f32[512]{0:T(512)S(1)} %fusion.84), kind=kOutput, calls=%fused_computation.14 | convolution fusion | flops 10148274176 | bytes 27992064 | tf_op jit(solution)/shard_map/dot_general | solution.py:343
  433.0 26.1 %mixer_fwd.3 = (f32[512,3072]{1,0:T(8,128)S(1)}, bf16[512,3072]{1,0:T(8,128)(2,1)S(1)}, f32[512,128]{1,0:T(8,128)S(1)}) custom-call(f32[24,8,512]{2,1,0:T(8,128)S(1)} %maximum_maximum_fusion.1.rows_ref, bf16[512,6448]{1,0:T(8,128)(2,1)} %convolution_convert_fusion.x_ref.z_ref.b_ref.c_ref, bf16[512,6448]{1,0:T(8,128)(2,1)} %convolution_convert_fusion.x_ref.z_ref.b_ref.c_ref, ...), custom_call_target="tpu_custom_call" | custom-call | flops 8000000000 | bytes 16000000 | tf_op jit(solution)/shard_map/mixer_fwd/pallas_call | solution.py:265
  483.9 62.7 %mixer_bwd.2 = (bf16[512,6528]{1,0:T(8,128)(2,1)}, f32[24,8,512]{2,1,0:T(8,128)S(1)}, f32[8,3072]{1,0:T(8,128)S(1)}, f32[8,256]{1,0:T(8,128)S(1)}) custom-call(f32[24,8,512]{2,1,0:T(8,128)S(1)} %maximum_maximum_fusion.1.rows_ref, bf16[512,6448]{1,0:T(8,128)(2,1)} %convolution_convert_fusion.x_ref.z_ref.b_ref.c_ref, ...), custom_call_target="tpu_custom_call" | custom-call | flops 16000000000 | bytes 40000000 | tf_op jit(solution)/shard_map/mixer_bwd/pallas_call | solution.py:293
  550.5 8.9 fusion
  568.3 8.9 fusion.2
  577.3 18.7 %fusion.20 = (f32[1536]{0:T(1024)S(1)}, f32[512]{0:T(512)S(1)}, bf16[512,1536]{1,0:T(8,128)(2,1)S(1)}) fusion(bf16[512,1536]{1,0:T(8,128)(2,1)} %get-tuple-element.157, f32[512]{0:T(512)S(1)} %fusion.84, f32[1536]{0:T(1024)S(1)} %mul.260, bf16[1536,6448]{0,1:T(8,128)(2,1)} %all-gather.10.cloned.1.call-done, bf16[512,6528]{1,0:T(8,128)(2,1)} %dynamic_update_slice.102), kind=kOutput, calls=%fused_computation.47 | convolution fusion | flops 10148902912 | bytes 29655040 | tf_op jit(solution)/shard_map/dot_general | solution.py:431
  617.4 63.3 %mixer_bwd.3 = (bf16[512,6528]{1,0:T(8,128)(2,1)}, f32[24,8,512]{2,1,0:T(8,128)S(1)}, f32[8,3072]{1,0:T(8,128)S(1)}, f32[8,256]{1,0:T(8,128)S(1)}) custom-call(f32[24,8,512]{2,1,0:T(8,128)S(1)} %maximum_maximum_fusion.rows_ref, bf16[512,6448]{1,0:T(8,128)(2,1)} %convolution_convert_fusion.1.x_ref.z_ref.b_ref.c_ref, ...), custom_call_target="tpu_custom_call" | custom-call | flops 16000000000 | bytes 40000000 | tf_op jit(solution)/shard_map/mixer_bwd/pallas_call | solution.py:293
  713.0 20.3 %fusion.21 = (f32[1536]{0:T(1024)S(1)}, f32[512]{0:T(512)S(1)}, bf16[512,1536]{1,0:T(8,128)(2,1)}) fusion(bf16[1,512,1536]{2,1,0:T(8,128)(2,1)S(1)} %copy-done.19, f32[512]{0:T(512)S(1)} %copy-done.66, f32[1536]{0:T(1024)S(1)} %copy-done.58, bf16[1536,6448]{0,1:T(8,128)(2,1)} %bitcast.255, bf16[512,6528]{1,0:T(8,128)(2,1)} %dynamic_update_slice.103), kind=kOutput, calls=%fused_computation.48 | convolution fusion | flops 10148902912 | bytes 29655040 | tf_op jit(solution)/shard_map/dot_general | solution.py:431
  742.6 12.4 collective-permute-done.42
  755.0 11.8 collective-permute-done.41
  773.5 51.8 %collective-permute-done.2 = f32[4,2,5348]{2,0,1:T(4,128)S(1)} collective-permute-done((f32[4,2,5348]{2,0,1:T(4,128)S(1)}, f32[4,2,5348]{2,0,1:T(4,128)S(1)}, u32[]{:S(2)}, u32[]{:S(2)}) %collective-permute-start.2) | collective-permute-done | bytes 171168 | tf_op jit(solution)/shard_map/ppermute | solution.py:470
  845.7 44.6 %reduce-scatter.11.cloned.1.call-done = bf16[384,2176]{1,0:T(8,128)(2,1)} async-done(((bf16[1536,2176]{1,0:T(8,128)(2,1)}), bf16[384,2176]{1,0:T(8,128)(2,1)}) %reduce-scatter.11.cloned.1.call-update) | async-done | bytes 1671184 | tf_op jit(solution)/shard_map/reduce_scatter | solution.py:396
  899.9 50.6 %reduce-scatter.15.cloned.1.call-done = bf16[384,2176]{1,0:T(8,128)(2,1)} async-done(((bf16[1536,2176]{1,0:T(8,128)(2,1)}), bf16[384,2176]{1,0:T(8,128)(2,1)}) %reduce-scatter.15.cloned.1.call-update) | async-done | bytes 1671184 | tf_op jit(solution)/shard_map/reduce_scatter | solution.py:396
  962.4 48.4 %reduce-scatter.17.cloned.1.call-done = bf16[384,2176]{1,0:T(8,128)(2,1)} async-done(((bf16[1536,2176]{1,0:T(8,128)(2,1)}), bf16[384,2176]{1,0:T(8,128)(2,1)}) %reduce-scatter.17.cloned.1.call-update) | async-done | bytes 1671184 | tf_op jit(solution)/shard_map/reduce_scatter | solution.py:396
  1046.6 11.1 collective-permute-done.20
  1066.0 10.1 collective-permute-done.21
  1077.5 15.9 %collective-permute-done.37 = f32[528,384]{1,0:T(8,128)} collective-permute-done((f32[528,384]{1,0:T(8,128)}, f32[528,384]{1,0:T(8,128)}, u32[]{:S(2)}, u32[]{:S(2)}) %collective-permute-start.37) | collective-permute-done | bytes 811040 | tf_op jit(solution)/shard_map/ppermute | solution.py:410
  1099.9 11.5 collective-permute-done.9
  1119.2 10.1 collective-permute-done.13
  1132.3 15.0 %collective-permute-done.15 = f32[544,384]{1,0:T(8,128)} collective-permute-done((f32[544,384]{1,0:T(8,128)}, f32[544,384]{1,0:T(8,128)}, u32[]{:S(2)}, u32[]{:S(2)}) %collective-permute-start.15) | collective-permute-done | bytes 835616 | tf_op jit(solution)/shard_map/ppermute | solution.py:410
  1148.7 16.4 %collective-permute-done.25 = f32[544,384]{1,0:T(8,128)} collective-permute-done((f32[544,384]{1,0:T(8,128)}, f32[544,384]{1,0:T(8,128)}, u32[]{:S(2)}, u32[]{:S(2)}) %collective-permute-start.25) | collective-permute-done | bytes 835616 | tf_op jit(solution)/shard_map/ppermute | solution.py:410
  1165.7 12.2 collective-permute-done.48
  1179.4 10.1 fusion.34
  1189.5 17.4 %collective-permute-done.47 = bf16[192,1536]{1,0:T(8,128)(2,1)S(1)} collective-permute-done((bf16[192,1536]{1,0:T(8,128)(2,1)}, bf16[192,1536]{1,0:T(8,128)(2,1)S(1)}, u32[]{:S(2)}, u32[]{:S(2)}) %collective-permute-start.47) | collective-permute-done | bytes 589856 | tf_op jit(solution)/shard_map/ppermute | solution.py:407
  1208.2 16.7 %collective-permute-done.46 = bf16[192,1536]{1,0:T(8,128)(2,1)S(1)} collective-permute-done((bf16[192,1536]{1,0:T(8,128)(2,1)}, bf16[192,1536]{1,0:T(8,128)(2,1)S(1)}, u32[]{:S(2)}, u32[]{:S(2)}) %collective-permute-start.46) | collective-permute-done | bytes 589856 | tf_op jit(solution)/shard_map/ppermute | solution.py:407
  1234.6 9.1 collective-permute-done.32
  (472 shorter events, 402.8 us)
Async XLA Ops:
  7.2 134.8 %all-gather.14.cloned.1.call-start = ((), (), s32[]{:S(2)}) async-start(), calls=%async_computation.19 | async-start | bytes 24760320 | tf_op jit(solution)/shard_map/all_gather | solution.py:389
  16.0 189.8 %all-gather.8.cloned.1.call-start = ((), (), s32[]{:S(2)}) async-start(), calls=%async_computation.8 | async-start | bytes 11796480 | tf_op jit(solution)/shard_map/all_gather | solution.py:389
  142.0 189.0 %all-gather.10.cloned.1.call-start = ((), (), s32[]{:S(2)}) async-start(), calls=%async_computation.9 | async-start | bytes 24760320 | tf_op jit(solution)/shard_map/all_gather | solution.py:389
  205.9 265.2 %all-gather.12.cloned.1.call-start = ((), (), s32[]{:S(2)}) async-start(), calls=%async_computation.10 | async-start | bytes 11796480 | tf_op jit(solution)/shard_map/all_gather | solution.py:389
  331.0 404.9 %reduce-scatter.21.cloned.1.call-start = ((), (), s32[]{:S(2)}) async-start(), calls=%async_computation.17 | async-start | bytes 11796480 | tf_op jit(solution)/shard_map/reduce_scatter | solution.py:396
  471.1 355.9 %reduce-scatter.13.cloned.1.call-start = ((), (), s32[]{:S(2)}) async-start(), calls=%async_computation.13 | async-start | bytes 8355840 | tf_op jit(solution)/shard_map/reduce_scatter | solution.py:396
  577.2 254.4 %reduce-scatter.19.cloned.1.call-start = ((), (), s32[]{:S(2)}) async-start(), calls=%async_computation.16 | async-start | bytes 8355840 | tf_op jit(solution)/shard_map/reduce_scatter | solution.py:396
  707.3 131.3 %reduce-scatter.9.cloned.1.call-start = ((), (), s32[]{:S(2)}) async-start(), calls=%async_computation.11 | async-start | bytes 8355840 | tf_op jit(solution)/shard_map/reduce_scatter | solution.py:396
  708.1 182.3 %reduce-scatter.11.cloned.1.call-start = ((), (), s32[]{:S(2)}) async-start(), calls=%async_computation.12 | async-start | bytes 8355840 | tf_op jit(solution)/shard_map/reduce_scatter | solution.py:396
  708.8 241.7 %reduce-scatter.15.cloned.1.call-start = ((), (), s32[]{:S(2)}) async-start(), calls=%async_computation.14 | async-start | bytes 8355840 | tf_op jit(solution)/shard_map/reduce_scatter | solution.py:396
  709.4 301.5 %reduce-scatter.17.cloned.1.call-start = ((), (), s32[]{:S(2)}) async-start(), calls=%async_computation.15 | async-start | bytes 8355840 | tf_op jit(solution)/shard_map/reduce_scatter | solution.py:396
  710.1 386.8 %reduce-scatter.23.cloned.1.call-start = ((), (), s32[]{:S(2)}) async-start(), calls=%async_computation.18 | async-start | bytes 11796480 | tf_op jit(solution)/shard_map/reduce_scatter | solution.py:396
  768.4 66.7 %collective-permute-start.43 = (f32[192,1536]{1,0:T(8,128)S(1)}, f32[192,1536]{1,0:T(8,128)S(1)}, u32[]{:S(2)}, u32[]{:S(2)}) collective-permute-start(f32[192,1536]{1,0:T(8,128)S(1)} %add_add_fusion.1), channel_id=1, source_target_pairs={{0,4},{4,0},{8,12},{12,8},{1,5},{5,1},{9,13},{13,9},{2,6},{6,2},{1... | collective-permute-start | bytes 3538952 | tf_op jit(solution)/shard_map/ppermute | solution.py:410
  769.9 67.0 %collective-permute-start.44 = (f32[192,1536]{1,0:T(8,128)S(1)}, f32[192,1536]{1,0:T(8,128)}, u32[]{:S(2)}, u32[]{:S(2)}) collective-permute-start(f32[192,1536]{1,0:T(8,128)S(1)} %add_add_fusion.1), channel_id=1, source_target_pairs={{0,8},{4,12},{8,0},{12,4},{1,9},{5,13},{9,1},{13,5},{2,10},{6,14},... | collective-permute-start | bytes 3538952 | tf_op jit(solution)/shard_map/ppermute | solution.py:410
  770.6 67.7 %collective-permute-start.45 = (f32[192,1536]{1,0:T(8,128)S(1)}, f32[192,1536]{1,0:T(8,128)}, u32[]{:S(2)}, u32[]{:S(2)}) collective-permute-start(f32[192,1536]{1,0:T(8,128)S(1)} %add_add_fusion.1), channel_id=1, source_target_pairs={{0,12},{4,8},{8,4},{12,0},{1,13},{5,9},{9,5},{13,1},{2,14},{6,10},... | collective-permute-start | bytes 3538952 | tf_op jit(solution)/shard_map/ppermute | solution.py:410
  835.1 60.8 %collective-permute-start.16 = (bf16[528,384]{0,1:T(8,128)(2,1)}, bf16[528,384]{0,1:T(8,128)(2,1)}, u32[]{:S(2)}, u32[]{:S(2)}) collective-permute-start(bf16[528,384]{0,1:T(8,128)(2,1)} %get-tuple-element.126), channel_id=1, source_target_pairs={{0,4},{4,0},{8,12},{12,8},{1,5},{5,1},{9,13},{13,9},{2,6},{6,2},{1... | collective-permute-start | bytes 1216520 | tf_op jit(solution)/shard_map/ppermute | solution.py:407
  899.4 62.8 %collective-permute-start.11 = (bf16[544,384]{0,1:T(8,128)(2,1)}, bf16[544,384]{0,1:T(8,128)(2,1)}, u32[]{:S(2)}, u32[]{:S(2)}) collective-permute-start(bf16[544,384]{0,1:T(8,128)(2,1)} %get-tuple-element.131), channel_id=1, source_target_pairs={{0,8},{4,12},{8,0},{12,4},{1,9},{5,13},{9,1},{13,5},{2,10},{6,14},... | collective-permute-start | bytes 1253384 | tf_op jit(solution)/shard_map/ppermute | solution.py:407
  955.2 62.1 %collective-permute-start.24 = (bf16[544,384]{0,1:T(8,128)(2,1)}, bf16[544,384]{0,1:T(8,128)(2,1)S(1)}, u32[]{:S(2)}, u32[]{:S(2)}) collective-permute-start(bf16[544,384]{0,1:T(8,128)(2,1)} %get-tuple-element.124), channel_id=1, source_target_pairs={{0,12},{4,8},{8,4},{12,0},{1,13},{5,9},{9,5},{13,1},{2,14},{6,10},... | collective-permute-start | bytes 1253384 | tf_op jit(solution)/shard_map/ppermute | solution.py:407
  956.7 62.0 %collective-permute-start.23 = (bf16[544,384]{0,1:T(8,128)(2,1)}, bf16[544,384]{0,1:T(8,128)(2,1)S(1)}, u32[]{:S(2)}, u32[]{:S(2)}) collective-permute-start(bf16[544,384]{0,1:T(8,128)(2,1)} %get-tuple-element.125), channel_id=1, source_target_pairs={{0,8},{4,12},{8,0},{12,4},{1,9},{5,13},{9,1},{13,5},{2,10},{6,14},... | collective-permute-start | bytes 1253384 | tf_op jit(solution)/shard_map/ppermute | solution.py:407
  957.2 61.9 %collective-permute-start.22 = (bf16[544,384]{0,1:T(8,128)(2,1)}, bf16[544,384]{0,1:T(8,128)(2,1)S(1)}, u32[]{:S(2)}, u32[]{:S(2)}) collective-permute-start(bf16[544,384]{0,1:T(8,128)(2,1)} %get-tuple-element.123), channel_id=1, source_target_pairs={{0,4},{4,0},{8,12},{12,8},{1,5},{5,1},{9,13},{13,9},{2,6},{6,2},{1... | collective-permute-start | bytes 1253384 | tf_op jit(solution)/shard_map/ppermute | solution.py:407
  962.2 83.8 %collective-permute-start.19 = (f32[528,384]{1,0:T(8,128)}, f32[528,384]{1,0:T(8,128)}, u32[]{:S(2)}, u32[]{:S(2)}) collective-permute-start(f32[528,384]{1,0:T(8,128)} %copy.131), channel_id=1, source_target_pairs={{0,4},{4,0},{8,12},{12,8},{1,5},{5,1},{9,13},{13,9},{2,6},{6,2},{1... | collective-permute-start | bytes 2433032 | tf_op jit(solution)/shard_map/ppermute | solution.py:410
  1030.1 63.9 %collective-permute-start.7 = (f32[544,384]{1,0:T(8,128)}, f32[544,384]{1,0:T(8,128)}, u32[]{:S(2)}, u32[]{:S(2)}) collective-permute-start(f32[544,384]{1,0:T(8,128)} %copy.123), channel_id=1, source_target_pairs={{0,4},{4,0},{8,12},{12,8},{1,5},{5,1},{9,13},{13,9},{2,6},{6,2},{1... | collective-permute-start | bytes 2506760 | tf_op jit(solution)/shard_map/ppermute | solution.py:410
  1096.4 68.7 %collective-permute-start.25 = (f32[544,384]{1,0:T(8,128)}, f32[544,384]{1,0:T(8,128)}, u32[]{:S(2)}, u32[]{:S(2)}) collective-permute-start(f32[544,384]{1,0:T(8,128)} %copy.135), channel_id=1, source_target_pairs={{0,4},{4,0},{8,12},{12,8},{1,5},{5,1},{9,13},{13,9},{2,6},{6,2},{1... | collective-permute-start | bytes 2506760 | tf_op jit(solution)/shard_map/ppermute | solution.py:410
  1111.4 66.5 %collective-permute-start.48 = (bf16[192,1536]{1,0:T(8,128)(2,1)}, bf16[192,1536]{1,0:T(8,128)(2,1)}, u32[]{:S(2)}, u32[]{:S(2)}) collective-permute-start(bf16[192,1536]{1,0:T(8,128)(2,1)} %get-tuple-element.112), channel_id=1, source_target_pairs={{0,12},{4,8},{8,4},{12,0},{1,13},{5,9},{9,5},{13,1},{2,14},{6,10},... | collective-permute-start | bytes 1769480 | tf_op jit(solution)/shard_map/ppermute | solution.py:407
  1129.3 99.7 %collective-permute-start.26 = (f32[544,384]{1,0:T(8,128)}, f32[544,384]{1,0:T(8,128)S(1)}, u32[]{:S(2)}, u32[]{:S(2)}) collective-permute-start(f32[544,384]{1,0:T(8,128)} %copy.135), channel_id=1, source_target_pairs={{0,8},{4,12},{8,0},{12,4},{1,9},{5,13},{9,1},{13,5},{2,10},{6,14},... | collective-permute-start | bytes 2506760 | tf_op jit(solution)/shard_map/ppermute | solution.py:410
  1129.9 99.7 %collective-permute-start.27 = (f32[544,384]{1,0:T(8,128)}, f32[544,384]{1,0:T(8,128)S(1)}, u32[]{:S(2)}, u32[]{:S(2)}) collective-permute-start(f32[544,384]{1,0:T(8,128)} %copy.135), channel_id=1, source_target_pairs={{0,12},{4,8},{8,4},{12,0},{1,13},{5,9},{9,5},{13,1},{2,14},{6,10},... | collective-permute-start | bytes 2506760 | tf_op jit(solution)/shard_map/ppermute | solution.py:410
  1147.2 83.8 %collective-permute-start.31 = (f32[544,384]{1,0:T(8,128)}, f32[544,384]{1,0:T(8,128)S(1)}, u32[]{:S(2)}, u32[]{:S(2)}) collective-permute-start(f32[544,384]{1,0:T(8,128)} %copy.139), channel_id=1, source_target_pairs={{0,4},{4,0},{8,12},{12,8},{1,5},{5,1},{9,13},{13,9},{2,6},{6,2},{1... | collective-permute-start | bytes 2506760 | tf_op jit(solution)/shard_map/ppermute | solution.py:410
  1229.0 149.7 %collective-permute-start.49 = (f32[192,1536]{1,0:T(8,128)}, f32[192,1536]{1,0:T(8,128)}, u32[]{:S(2)}, u32[]{:S(2)}) collective-permute-start(f32[192,1536]{1,0:T(8,128)} %add_add_fusion), channel_id=1, source_target_pairs={{0,4},{4,0},{8,12},{12,8},{1,5},{5,1},{9,13},{13,9},{2,6},{6,2},{1... | collective-permute-start | bytes 3538952 | tf_op jit(solution)/shard_map/ppermute | solution.py:410
  1229.6 153.5 %collective-permute-start.50 = (f32[192,1536]{1,0:T(8,128)}, f32[192,1536]{1,0:T(8,128)}, u32[]{:S(2)}, u32[]{:S(2)}) collective-permute-start(f32[192,1536]{1,0:T(8,128)} %add_add_fusion), channel_id=1, source_target_pairs={{0,8},{4,12},{8,0},{12,4},{1,9},{5,13},{9,1},{13,5},{2,10},{6,14},... | collective-permute-start | bytes 3538952 | tf_op jit(solution)/shard_map/ppermute | solution.py:410
  1231.1 156.5 %collective-permute-start.51 = (f32[192,1536]{1,0:T(8,128)}, f32[192,1536]{1,0:T(8,128)}, u32[]{:S(2)}, u32[]{:S(2)}) collective-permute-start(f32[192,1536]{1,0:T(8,128)} %add_add_fusion), channel_id=1, source_target_pairs={{0,12},{4,8},{8,4},{12,0},{1,13},{5,9},{9,5},{13,1},{2,14},{6,10},... | collective-permute-start | bytes 3538952 | tf_op jit(solution)/shard_map/ppermute | solution.py:410
  1243.8 123.8 %collective-permute-start.38 = (f32[528,384]{1,0:T(8,128)}, f32[528,384]{1,0:T(8,128)}, u32[]{:S(2)}, u32[]{:S(2)}) collective-permute-start(f32[528,384]{1,0:T(8,128)} %copy.143), channel_id=1, source_target_pairs={{0,8},{4,12},{8,0},{12,4},{1,9},{5,13},{9,1},{13,5},{2,10},{6,14},... | collective-permute-start | bytes 2433032 | tf_op jit(solution)/shard_map/ppermute | solution.py:410
  1247.3 123.9 %collective-permute-start.39 = (f32[528,384]{1,0:T(8,128)}, f32[528,384]{1,0:T(8,128)}, u32[]{:S(2)}, u32[]{:S(2)}) collective-permute-start(f32[528,384]{1,0:T(8,128)} %copy.143), channel_id=1, source_target_pairs={{0,12},{4,8},{8,4},{12,0},{1,13},{5,9},{9,5},{13,1},{2,14},{6,10},... | collective-permute-start | bytes 2433032 | tf_op jit(solution)/shard_map/ppermute | solution.py:410
  (109 other events, 3873.7 us)
Sparse Core Ops, SparseCore 0:
  16.2 125.7 all-gather.13
  143.5 62.3 all-gather.7
  208.0 122.9 all-gather.9
  332.4 62.3 all-gather.11
  471.2 74.5 reduce-scatter.20
  577.3 58.1 reduce-scatter.12
  707.4 62.1 reduce-scatter.18
  772.2 57.7 reduce-scatter.8
  832.6 57.7 reduce-scatter.10
  892.7 57.7 reduce-scatter.14
  953.1 57.7 reduce-scatter.16
  1013.9 74.1 reduce-scatter.22

commit v2 on v1

--- a/solution.py
+++ b/solution.py
@@ -6,9 +6,11 @@
 from jax.sharding import PartitionSpec as P
 
 
+ALL = Ellipsis
 CHUNK = 256
 SEQ = 512
 LANES = 128
+PAD = 8
 HEAD = 64
 D_MODEL = 1536
 D_INNER = 3072
@@ -32,41 +34,44 @@
     return lax.dot_general(a, b, dims, preferred_element_type=F32)
 
 
+def _sum(x, axis):
+    return jnp.sum(x, axis=axis, keepdims=True)
+
+
 def _iota(shape, dim):
     return lax.broadcasted_iota(jnp.int32, shape, dim)
 
 
-def _later(x, k):
-    if k == 0:
-        return x
-    return jnp.where(_iota(x.shape, 0) >= k, pltpu.roll(x, k, 0), 0.0)
-
-
-def _sooner(x, k):
-    if k == 0:
-        return x
-    n = x.shape[0]
-    return jnp.where(_iota(x.shape, 0) < n - k, pltpu.roll(x, n - k, 0), 0.0)
-
-
-def _conv(x_in, taps):
-    out = taps[4:5] + x_in * taps[3:4]
+def _fill(pad, x):
+    zeros = jnp.zeros((PAD, LANES), F32)
+    pad[pl.ds(0, PAD), :] = zeros
+    pad[pl.ds(PAD, SEQ), :] = x
+    pad[pl.ds(PAD + SEQ, PAD), :] = zeros
+
+
+def _shift(pad, k):
+    return pad[pl.ds(PAD + k, SEQ), :]
+
+
+def _conv(pad, taps):
+    out = taps[4:5] + _shift(pad, 0) * taps[3:4]
     for k in range(3):
-        out += _later(x_in, 3 - k) * taps[k:k + 1]
+        out += _shift(pad, k - 3) * taps[k:k + 1]
     return out
 
 
-def _conv_back(d_out, x_in, taps):
+def _conv_back(pad_out, d_out, pad_in, taps):
+    _fill(pad_out, d_out)
     d_in = d_out * taps[3:4]
     for k in range(3):
-        d_in += _sooner(d_out, 3 - k) * taps[k:k + 1]
-    rows = [jnp.sum(d_out * _later(x_in, 3 - k), axis=0, keepdims=True) for k in range(4)]
-    rows.append(jnp.sum(d_out, axis=0, keepdims=True))
+        d_in += _shift(pad_out, 3 - k) * taps[k:k + 1]
+    rows = [_sum(d_out * _shift(pad_in, k - 3), 0) for k in range(4)]
+    rows.append(_sum(d_out, 0))
     return d_in, rows
 
 
 def _sigmoid(x):
-    return 1.0 / (1.0 + jnp.exp(-x))
+    return 0.5 * jnp.tanh(0.5 * x) + 0.5
 
 
 def _silu_grad(x, sig):
@@ -78,10 +83,11 @@
     return jnp.where(_iota(shape, 1) < HEAD, a, b)
 
 
-def _scores(b_ref, c_ref, tb_ref, tc_ref, b_sc, c_sc, g_sc):
+def _scores(b_ref, c_ref, tb_ref, tc_ref, b_sc, c_sc, g_sc, pad):
     for ref, taps, dst in ((b_ref, tb_ref, b_sc), (c_ref, tc_ref, c_sc)):
-        pre = _conv(ref[...].astype(F32), taps[...])
-        dst[...] = (pre * _sigmoid(pre)).astype(BF16)
+        _fill(pad, ref[ALL].astype(F32))
+        pre = _conv(pad, taps[ALL])
+        dst[ALL] = (pre * _sigmoid(pre)).astype(BF16)
     causal = _iota((CHUNK, CHUNK), 0) >= _iota((CHUNK, CHUNK), 1)
     for c in range(2):
         sl = pl.ds(c * CHUNK, CHUNK)
@@ -102,17 +108,18 @@
 
 
 def fwd_kernel(rows_ref, x_ref, z_ref, b_ref, c_ref, tx_ref, tb_ref, tc_ref, par_ref,
-               y_ref, n_ref, r_ref, b_sc, c_sc, g_sc, v_sc, acc):
+               y_ref, n_ref, r_ref, b_sc, c_sc, g_sc, v_sc, acc, pad):
     j = pl.program_id(0)
 
     @pl.when(j == 0)
     def _():
-        _scores(b_ref, c_ref, tb_ref, tc_ref, b_sc, c_sc, g_sc)
-        acc[...] = jnp.zeros_like(acc)
+        _scores(b_ref, c_ref, tb_ref, tc_ref, b_sc, c_sc, g_sc, pad)
+        acc[ALL] = jnp.zeros_like(acc)
 
     rows = rows_ref[0]
     cols = rows.T
-    pre = _conv(x_ref[...].astype(F32), tx_ref[...])
+    _fill(pad, x_ref[ALL].astype(F32))
+    pre = _conv(pad, tx_ref[ALL])
     x = pre * _sigmoid(pre)
     x_dt = x * _pair(cols[:, 0:1], cols[:, 1:2])
     x_b = x_dt.astype(BF16)
@@ -126,17 +133,17 @@
     y_parts[1] += from_start * _dot_dims(c_sc[pl.ds(CHUNK, CHUNK), :], state, NT)
     lane0 = pl.multiple_of(j * LANES, LANES)
     y = jnp.concatenate(y_parts, axis=0) + par_ref[1:2, pl.ds(lane0, LANES)] * x
-    y_ref[...] = y
-    z = z_ref[...].astype(F32)
+    y_ref[ALL] = y
+    z = z_ref[ALL].astype(F32)
     v = y * (z * _sigmoid(z))
     v_sc[j] = v
-    acc[...] += v * v
+    acc[ALL] += v * v
 
     @pl.when(j == N_PAIRS - 1)
     def _():
-        r = lax.rsqrt(jnp.sum(acc[...], axis=1, keepdims=True) / D_INNER + NORM_EPS)
+        r = lax.rsqrt(_sum(acc[ALL], 1) / D_INNER + NORM_EPS)
         r_full = jnp.broadcast_to(r, (SEQ, LANES))
-        r_ref[...] = r_full
+        r_ref[ALL] = r_full
 
         @pl.loop(0, N_PAIRS)
         def _(i):
@@ -145,55 +152,55 @@
 
 
 def bwd_kernel(rows_ref, x_ref, z_ref, b_ref, c_ref, y_ref, dn_ref, r_ref, tx_ref, tb_ref, tc_ref, par_ref,
-               dp_ref, drows_ref, gch_ref, gbc_ref, b_sc, c_sc, g_sc, dg_sc, dc_sc, db_sc, acc):
+               dp_ref, drows_ref, gch_ref, gbc_ref, b_sc, c_sc, g_sc, dg_sc, dc_sc, db_sc, acc, pad, pad_out):
     phase, j = pl.program_id(0), pl.program_id(1)
     gate = par_ref[0:1]
     skip = par_ref[1:2]
-    z = z_ref[...].astype(F32)
+    z = z_ref[ALL].astype(F32)
     sig_z = _sigmoid(z)
     act_z = z * sig_z
-    y = y_ref[...]
+    y = y_ref[ALL]
     v = y * act_z
-    d_n = dn_ref[...].astype(F32)
+    d_n = dn_ref[ALL].astype(F32)
     d_vn = d_n * gate
 
     @pl.when(phase == 0)
     def _():
         @pl.when(j == 0)
         def _():
-            acc[...] = jnp.zeros_like(acc)
-
-        acc[...] += d_vn * v
+            acc[ALL] = jnp.zeros_like(acc)
+
+        acc[ALL] += d_vn * v
 
     @pl.when(phase == 1)
     def _():
         @pl.when(j == 0)
         def _():
-            total = jnp.sum(acc[...], axis=1, keepdims=True) / D_INNER
-            acc[...] = jnp.broadcast_to(total, (SEQ, LANES))
-            _scores(b_ref, c_ref, tb_ref, tc_ref, b_sc, c_sc, g_sc)
-            dg_sc[...] = jnp.zeros_like(dg_sc)
-            dc_sc[...] = jnp.zeros_like(dc_sc)
-            db_sc[...] = jnp.zeros_like(db_sc)
-
-        r = r_ref[...]
-        d_v = r * d_vn - v * (r * r * r) * acc[...]
-        g_gate = jnp.sum(d_n * v * r, axis=0, keepdims=True)
+            total = _sum(acc[ALL], 1) / D_INNER
+            acc[ALL] = jnp.broadcast_to(total, (SEQ, LANES))
+            _scores(b_ref, c_ref, tb_ref, tc_ref, b_sc, c_sc, g_sc, pad)
+            dg_sc[ALL] = jnp.zeros_like(dg_sc)
+            dc_sc[ALL] = jnp.zeros_like(dc_sc)
+            db_sc[ALL] = jnp.zeros_like(db_sc)
+
+        r = r_ref[ALL]
+        d_v = r * d_vn - v * (r * r * r) * acc[ALL]
+        g_gate = _sum(d_n * v * r, 0)
         lane0 = pl.multiple_of(j * LANES, LANES)
         dp_ref[:, pl.ds(lane0, LANES)] = (d_v * y * _silu_grad(z, sig_z)).astype(BF16)
         d_y = d_v * act_z
 
         rows = rows_ref[0]
         cols = rows.T
-        x_in = x_ref[...].astype(F32)
-        pre = _conv(x_in, tx_ref[...])
+        _fill(pad, x_ref[ALL].astype(F32))
+        pre = _conv(pad, tx_ref[ALL])
         sig_x = _sigmoid(pre)
         x = pre * sig_x
         dt = _pair(cols[:, 0:1], cols[:, 1:2])
         x_dt = x * dt
         x_b = x_dt.astype(BF16)
         x_r = x_b.astype(F32)
-        g_skip = jnp.sum(d_y * x, axis=0, keepdims=True)
+        g_skip = _sum(d_y * x, 0)
         dy_b = d_y.astype(BF16)
         dy_r = dy_b.astype(F32)
         dy_t = dy_r.T.astype(BF16)
@@ -212,24 +219,24 @@
             dx_parts.append(jnp.concatenate(halves, axis=0).T)
         state, x_end, weight = _state(x_dt, rows, cols, b_sc)
         dy_off = dy_r[CHUNK:] * jnp.exp(_pair(cols[CHUNK:, 2:3], cols[CHUNK:, 3:4]))
-        dc_sc[...] += _dot(dy_off.astype(BF16), state)
+        dc_sc[ALL] += _dot(dy_off.astype(BF16), state)
         d_state = _dot(dy_off.T.astype(BF16), c_sc[pl.ds(CHUNK, CHUNK), :]).astype(BF16)
-        db_sc[...] += _dot(x_end, d_state)
+        db_sc[ALL] += _dot(x_end, d_state)
         dx_state = weight * _dot_dims(b_sc[pl.ds(0, CHUNK), :], d_state, NT)
         dx_parts[0] += dx_state
         d_xdt = jnp.concatenate(dx_parts, axis=0)
-        end_sum = jnp.sum(x_r[:CHUNK] * dx_state, axis=0, keepdims=True)
+        end_sum = _sum(x_r[:CHUNK] * dx_state, 0)
         d_cum = dy_r * (y - skip * x) - x_r * d_xdt
         d_cum += jnp.where(_iota((SEQ, LANES), 0) == CHUNK - 1, end_sum, 0.0)
         dt_t = (d_xdt * x).T
         cum_t = d_cum.T
         drows_ref[0] = jnp.concatenate(
-            [jnp.sum(part[h * HEAD:(h + 1) * HEAD], axis=0, keepdims=True) for part in (dt_t, cum_t) for h in range(2)]
+            [_sum(part[h * HEAD:(h + 1) * HEAD], 0) for part in (dt_t, cum_t) for h in range(2)]
             + [jnp.zeros((4, SEQ), F32)], axis=0)
         d_pre = (d_xdt * dt + skip * d_y) * _silu_grad(pre, sig_x)
-        d_in, g_rows = _conv_back(d_pre, x_in, tx_ref[...])
+        d_in, g_rows = _conv_back(pad_out, d_pre, pad, tx_ref[ALL])
         dp_ref[:, pl.ds(pl.multiple_of(D_INNER + lane0, LANES), LANES)] = d_in.astype(BF16)
-        gch_ref[...] = jnp.concatenate(g_rows + [g_gate, g_skip, jnp.zeros((1, LANES), F32)], axis=0)
+        gch_ref[ALL] = jnp.concatenate(g_rows + [g_gate, g_skip, jnp.zeros((1, LANES), F32)], axis=0)
 
         @pl.when(j == N_PAIRS - 1)
         def _():
@@ -240,13 +247,13 @@
                 d_g = jnp.where(causal, dg_sc[c], 0.0)
                 d_c.append(_dot(d_g.astype(BF16), b_sc[sl, :]))
                 d_b.append(_dot(d_g.T.astype(BF16), c_sc[sl, :]))
-            d_c[1] += dc_sc[...]
-            d_b[0] += db_sc[...]
+            d_c[1] += dc_sc[ALL]
+            d_b[0] += db_sc[ALL]
             for i, (parts, ref, taps) in enumerate(((d_b, b_ref, tb_ref), (d_c, c_ref, tc_ref))):
-                val = ref[...].astype(F32)
-                pre_i = _conv(val, taps[...])
+                _fill(pad, ref[ALL].astype(F32))
+                pre_i = _conv(pad, taps[ALL])
                 d_pre_i = jnp.concatenate(parts, axis=0) * _silu_grad(pre_i, _sigmoid(pre_i))
-                d_val, g_val = _conv_back(d_pre_i, val, taps[...])
+                d_val, g_val = _conv_back(pad_out, d_pre_i, pad, taps[ALL])
                 dp_ref[:, pl.ds(2 * D_INNER + i * LANES, LANES)] = d_val.astype(BF16)
                 gbc_ref[:, pl.ds(i * LANES, LANES)] = jnp.concatenate(g_val + [jnp.zeros((3, LANES), F32)], axis=0)
             dp_ref[:, pl.ds(2 * D_INNER + 2 * LANES, LANES)] = jnp.zeros((SEQ, LANES), BF16)
@@ -254,10 +261,6 @@
 
 def _col(block):
     return pl.BlockSpec((SEQ, LANES), lambda j: (0, block(j)))
-
-
-def part_rows(rows):
-    return -(-rows // 64) * 16
 
 
 def mixer_fwd(proj, rows, taps, par):
@@ -279,7 +282,7 @@
         ],
         scratch_shapes=[
             pltpu.VMEM((SEQ, LANES), BF16), pltpu.VMEM((SEQ, LANES), BF16), pltpu.VMEM((2, CHUNK, CHUNK), F32),
-            pltpu.VMEM((N_PAIRS, SEQ, LANES), F32), pltpu.VMEM((SEQ, LANES), F32),
+            pltpu.VMEM((N_PAIRS, SEQ, LANES), F32), pltpu.VMEM((SEQ, LANES), F32), pltpu.VMEM((SEQ + 2 * PAD, LANES), F32),
         ],
         compiler_params=pltpu.CompilerParams(dimension_semantics=("arbitrary",), vmem_limit_bytes=40 * 2 ** 20),
         cost_estimate=pl.CostEstimate(flops=8 * 10 ** 9, bytes_accessed=16 * 10 ** 6, transcendentals=10 ** 7),
@@ -314,12 +317,182 @@
         scratch_shapes=[
             pltpu.VMEM((SEQ, LANES), BF16), pltpu.VMEM((SEQ, LANES), BF16), pltpu.VMEM((2, CHUNK, CHUNK), F32),
             pltpu.VMEM((2, CHUNK, CHUNK), F32), pltpu.VMEM((CHUNK, LANES), F32), pltpu.VMEM((CHUNK, LANES), F32),
-            pltpu.VMEM((SEQ, LANES), F32),
+            pltpu.VMEM((SEQ, LANES), F32), pltpu.VMEM((SEQ + 2 * PAD, LANES), F32), pltpu.VMEM((SEQ + 2 * PAD, LANES), F32),
         ],
         compiler_params=pltpu.CompilerParams(dimension_semantics=("arbitrary", "arbitrary"), vmem_limit_bytes=40 * 2 ** 20),
         cost_estimate=pl.CostEstimate(flops=16 * 10 ** 9, bytes_accessed=40 * 10 ** 6, transcendentals=10 ** 7),
         name="mixer_bwd",
     )(rows, proj, proj, proj, proj, y, d_n, r, taps, taps, taps, par)
+
+
+IN_PART = 800
+OUT_PART = 192
+UNITS = ((0, 0, IN_PART), (0, 4 * IN_PART, IN_PART), (1, 0, OUT_PART))
+N_UNITS = 2 * len(UNITS)
+
+
+def gather_kernel(win_ref, wout_ref, in_a, out_a, in_b, out_b, buf_in, buf_out, sends, recvs, tails, tailr, loads, stores):
+    i, d = lax.axis_index('fsdp'), lax.axis_index('dp')
+    x, c, z, y = i // 2, i % 2, d // 2, d % 2
+    chip_x, core = 2 * (1 - x) + c, 2 * x + (1 - c)
+    near_y, near_z = 2 * z + (1 - y), 2 * (1 - z) + y
+    to_x, to_core = {'dp': d, 'fsdp': chip_x}, {'dp': d, 'fsdp': core}
+    to_y, to_z = {'dp': near_y, 'fsdp': i}, {'dp': near_z, 'fsdp': i}
+
+    barrier = pltpu.get_barrier_semaphore()
+    for device in (to_x, to_core, to_y, to_z):
+        pl.semaphore_signal(barrier, inc=1, device_id=device, device_id_type=pl.DeviceIdType.MESH)
+    pl.semaphore_wait(barrier, 4)
+
+    fulls = ((in_a, out_a), (in_b, out_b))
+    pieces, bufs = (win_ref, wout_ref), (buf_in, buf_out)
+
+    def source(u, row, size):
+        layer, (kind, _, _) = u // 3, UNITS[u % 3]
+        return pieces[kind].at[layer, pl.ds(row, size), :]
+
+    def place(u, piece, row, size):
+        layer, (kind, _, _) = u // 3, UNITS[u % 3]
+        if kind == 0:
+            return fulls[layer][0].at[pl.ds(row, size), pl.ds(pl.multiple_of(piece * 384, 128), 384)]
+        return fulls[layer][1].at[pl.ds(pl.multiple_of(piece * 768 + row, 16), size), :]
+
+    def span(u, q):
+        _, first, size = UNITS[u % 3]
+        return pl.multiple_of(first + q * size, 16), size
+
+    def copy(u, slot, src, dst, device):
+        return pltpu.make_async_remote_copy(
+            src_ref=src, dst_ref=dst, send_sem=sends.at[u, slot], recv_sem=recvs.at[u, slot],
+            device_id=device, device_id_type=pl.DeviceIdType.MESH)
+
+    def forward(u, slot, piece, row, size, device):
+        return copy(u, slot, place(u, piece, row, size), place(u, piece, row, size), device)
+
+    started = []
+
+    def go(op):
+        op.start()
+        started.append(op)
+
+    def tail_copy(layer, slot, src, device):
+        dst = fulls[layer][0].at[pl.ds(8 * IN_PART, N_HEADS), pl.ds(pl.multiple_of((i if slot < 2 else chip_x) * 384, 128), 384)]
+        return pltpu.make_async_remote_copy(
+            src_ref=src, dst_ref=dst, send_sem=tails.at[layer, slot], recv_sem=tailr.at[layer, slot],
+            device_id=device, device_id_type=pl.DeviceIdType.MESH)
+
+    for u in range(N_UNITS):
+        row, size = span(u, d)
+        go(copy(u, 0, source(u, row, size), place(u, i, row, size), to_x))
+    tails_own = []
+    for layer in range(2):
+        src = win_ref.at[layer, pl.ds(8 * IN_PART, N_HEADS), :]
+        for slot, device in ((0, to_x), (1, to_core)):
+            op = tail_copy(layer, slot, src, device)
+            op.start()
+            tails_own.append(op)
+    for u in range(N_UNITS):
+        _, first, size = UNITS[u % 3]
+        go(copy(u, 5, source(u, first, 4 * size), place(u, i, first, 4 * size), to_core))
+
+    local_in = [pltpu.make_async_copy(pieces[kind].at[layer], bufs[kind].at[layer], loads.at[layer, kind])
+                for layer in range(2) for kind in range(2)]
+    for op in local_in:
+        op.start()
+    local_out = []
+    for n, op in enumerate(local_in):
+        layer, kind = n // 2, n % 2
+        op.wait()
+        if kind == 0:
+            dst = fulls[layer][0].at[:, pl.ds(pl.multiple_of(i * 384, 128), 384)]
+        else:
+            dst = fulls[layer][1].at[pl.ds(pl.multiple_of(i * 768, 16), 768), :]
+        out = pltpu.make_async_copy(bufs[kind].at[layer], dst, stores.at[layer, kind])
+        out.start()
+        local_out.append(out)
+
+    def got(u, slot, piece, row, size):
+        forward(u, slot, piece, row, size, to_core).wait_recv()
+
+    def stage_one(u):
+        row, size = span(u, d)
+        got(u, 0, chip_x, row, size)
+        go(forward(u, 1, chip_x, row, size, to_y))
+        go(forward(u, 2, chip_x, row, size, to_z))
+        go(forward(u, 6, chip_x, row, size, to_core))
+
+    def stage_two(u):
+        half = UNITS[u % 3][2] // 2
+        row, size = span(u, near_y)
+        got(u, 1, chip_x, row, size)
+        go(forward(u, 3, chip_x, row, half, to_z))
+        go(forward(u, 7, chip_x, row, size, to_core))
+        row, size = span(u, near_z)
+        got(u, 2, chip_x, row, size)
+        go(forward(u, 4, chip_x, row + half, half, to_y))
+        go(forward(u, 8, chip_x, row, size, to_core))
+
+    def stage_three(u):
+        half = UNITS[u % 3][2] // 2
+        row, _ = span(u, 2 * (1 - z) + (1 - y))
+        got(u, 3, chip_x, row, half)
+        go(forward(u, 9, chip_x, row, half, to_core))
+        got(u, 4, chip_x, row + half, half)
+        go(forward(u, 10, chip_x, row + half, half, to_core))
+
+    for t in range(N_UNITS + 2):
+        if t < N_UNITS:
+            stage_one(t)
+        if 0 <= t - 1 < N_UNITS:
+            stage_two(t - 1)
+        if 0 <= t - 2:
+            stage_three(t - 2)
+
+    for layer in range(2):
+        tail_at = fulls[layer][0].at[pl.ds(8 * IN_PART, N_HEADS), pl.ds(pl.multiple_of(chip_x * 384, 128), 384)]
+        tail_copy(layer, 0, win_ref.at[layer, pl.ds(8 * IN_PART, N_HEADS), :], to_x).wait_recv()
+        op = tail_copy(layer, 2, tail_at, to_core)
+        op.start()
+        tails_own.append(op)
+
+    diag, other_core_x = 2 * (1 - z) + (1 - y), 2 * (1 - x) + (1 - c)
+    for u in range(N_UNITS):
+        _, first, size = UNITS[u % 3]
+        half = size // 2
+        got(u, 5, core, first, 4 * size)
+        for slot, q in ((6, d), (7, near_y), (8, near_z)):
+            row, _ = span(u, q)
+            got(u, slot, other_core_x, row, size)
+        row, _ = span(u, diag)
+        got(u, 9, other_core_x, row, half)
+        got(u, 10, other_core_x, row + half, half)
+    for layer in range(2):
+        for slot in (1, 2):
+            tail_copy(layer, slot, win_ref.at[layer, pl.ds(8 * IN_PART, N_HEADS), :], to_core).wait_recv()
+    for op in started + tails_own:
+        op.wait_send()
+    for op in local_out:
+        op.wait()
+
+
+def gather_weights(w_in_t, w_out):
+    full = [jax.ShapeDtypeStruct((PROJ, D_MODEL), BF16), jax.ShapeDtypeStruct((D_INNER, D_MODEL), BF16)]
+    hbm = pl.BlockSpec(memory_space=pltpu.HBM)
+    return pl.pallas_call(
+        gather_kernel,
+        in_specs=[hbm, hbm],
+        out_specs=[hbm] * 4,
+        out_shape=full + full,
+        scratch_shapes=[
+            pltpu.VMEM(w_in_t.shape, BF16), pltpu.VMEM(w_out.shape, BF16),
+            pltpu.SemaphoreType.DMA((N_UNITS, 11)), pltpu.SemaphoreType.DMA((N_UNITS, 11)),
+            pltpu.SemaphoreType.DMA((2, 3)), pltpu.SemaphoreType.DMA((2, 3)),
+            pltpu.SemaphoreType.DMA((2, 2)), pltpu.SemaphoreType.DMA((2, 2)),
+        ],
+        compiler_params=pltpu.CompilerParams(collective_id=0, has_side_effects=True, vmem_limit_bytes=40 * 2 ** 20),
+        cost_estimate=pl.CostEstimate(flops=10 ** 9, bytes_accessed=10 ** 8, transcendentals=0),
+        name="gather_weights",
+    )(w_in_t, w_out)
 
 
 def pre_norm(u_rows, norm_w):
@@ -340,7 +513,7 @@
 def layer_forward(u_rows, small, w_in, w_out):
     norm_w, taps, par, dt_bias, a_log = small
     h_norm, norm_pull = jax.vjp(pre_norm, u_rows, norm_w)
-    proj = jnp.dot(h_norm, w_in, preferred_element_type=F32).astype(BF16)
+    proj = lax.dot_general(h_norm, w_in, NT, preferred_element_type=F32).astype(BF16)
     rows, rows_pull = jax.vjp(head_rows, proj[:, 2 * D_INNER + 2 * LANES:], dt_bias, a_log)
     y, y_norm, r = mixer_fwd(proj, rows, taps, par)
     out = (u_rows.astype(F32) + jnp.dot(y_norm, w_out, preferred_element_type=F32)).astype(BF16)
@@ -365,6 +538,7 @@
         widths = [piece.shape[1] for piece in small_pieces]
         packed = jnp.concatenate([piece.astype(F32) for piece in small_pieces], axis=1)
         gathered = lax.all_gather(packed, 'fsdp', axis=0)
+        w_in, w_out, gathered = lax.optimization_barrier((w_in, w_out, gathered))
 
         def small_layer(layer):
             vals, at = [], 0
@@ -380,55 +554,54 @@
                 jnp.zeros((6, D_INNER), F32)], axis=0)
             return norm.reshape(D_MODEL), taps, par, bias.reshape(N_HEADS), alog.reshape(N_HEADS)
 
-        def gather_in_order(pieces):
-            full, fulls = None, []
-            for piece in pieces:
-                if full is not None:
-                    piece, full = lax.optimization_barrier((piece, full))
-                    fulls.append(full)
-                full = lax.all_gather(piece, 'fsdp', axis=0, tiled=True)
-            return fulls + [full]
+        chip, core = me_fsdp // 2, me_fsdp % 2
+        swap = lambda k: [(i, i ^ k) for i in range(4)]
+
+        def by_core(left):
+            size = left.shape[1] // 4
+            return [jnp.concatenate([lax.dynamic_slice_in_dim(left, (2 * half + at) * size, size, 1) for half in range(2)], axis=1)
+                    for at in (1 - core, core)]
 
         def partial_grad(left, right):
             return (lax.dot_general(left, right, TN, preferred_element_type=F32) / batch_tot).astype(BF16)
 
-        def spread(part, flip=False, valid=None):
-            piece = lax.psum_scatter(part, 'fsdp', scatter_dimension=0, tiled=True)
-            piece = piece.T if flip else piece
-            rows = piece.shape[0] if valid is None else valid
-            size = part_rows(rows)
-
-            def quarter(k):
-                return lax.dynamic_slice_in_dim(piece, jnp.minimum((me_dp ^ k) * size, rows - size), size, 0)
-
-            sent = [quarter(k) for k in range(dp_size)]
-            terms = sent[:1]
+        def spread(sent, kept, axis):
+            got = lax.ppermute(sent, 'fsdp', swap(1))
+            chip_u, got = lax.optimization_barrier((chip, got))
+            pair = kept + got
+            size = pair.shape[axis] // 2
+            got = lax.ppermute(lax.dynamic_slice_in_dim(pair, (1 - chip_u) * size, size, axis), 'fsdp', swap(2))
+            dp_u, got = lax.optimization_barrier((me_dp, got))
+            piece = lax.dynamic_slice_in_dim(pair, chip_u * size, size, axis) + got
+            quarters = piece.reshape(dp_size, piece.shape[0] // dp_size, piece.shape[1])
+            terms = [lax.dynamic_index_in_dim(quarters, dp_u ^ k, 0, keepdims=False) for k in range(dp_size)]
             for k in range(1, dp_size):
-                terms.append(lax.ppermute(sent[k], 'dp', [(i, i ^ k) for i in range(dp_size)]))
+                terms[k] = lax.ppermute(terms[k], 'dp', swap(k))
             terms = [term.astype(F32) for term in terms]
             total = (terms[0] + terms[1]) + (terms[2] + terms[3])
-            return [total] + [lax.ppermute(total, 'dp', [(i, i ^ k) for i in range(dp_size)]) for k in range(1, dp_size)]
-
-        def place(buf, layer, parts, first, rows):
-            for k, part in enumerate(parts):
-                row = first + jnp.minimum((me_dp ^ k) * part.shape[0], rows - part.shape[0])
-                buf = lax.dynamic_update_slice(buf, part[None], (layer, row, 0))
-            return buf
+            return lax.all_gather(total, 'dp', axis=0, tiled=True)
 
         def layer_backward(d_out, saved, small, full_in, full_out):
             _, taps, par, _, _ = small
             h_norm, norm_pull, proj, rows, rows_pull, y, y_norm, r = saved
-            g_out_part = partial_grad(y_norm, d_out)
-            d_out, g_out_part = lax.optimization_barrier((d_out, g_out_part))
-            out_parts = spread(g_out_part)
+            y_other, y_own = by_core(y_norm)
+            sent = partial_grad(y_other, d_out)
+            d_out, sent = lax.optimization_barrier((d_out, sent))
+            out_parts = spread(sent, partial_grad(y_own, d_out), 0)
             d_n = lax.dot_general(d_out, full_out, NT, preferred_element_type=F32).astype(BF16)
             d_proj, d_rows, g_ch, g_bc = mixer_bwd(proj, rows, taps, par, y, d_n, r)
             d_raw, g_bias, g_alog = rows_pull(d_rows)
             d_proj = lax.dynamic_update_slice(d_proj, d_raw, (0, 2 * D_INNER + 2 * LANES))
-            g_in_parts = [partial_grad(h_norm, d_proj[:, lo:hi]) for lo, hi in COL_CHUNKS]
-            d_proj, g_in_parts = lax.optimization_barrier((d_proj, g_in_parts))
-            in_parts = [spread(part, flip=True, valid=min(hi, PROJ) - lo) for part, (lo, hi) in zip(g_in_parts, COL_CHUNKS)]
-            d_h = lax.dot_general(d_proj[:, :PROJ], full_in, NT, preferred_element_type=F32).astype(BF16)
+            h_other, h_own = by_core(h_norm)
+            cols = [d_proj[:, lo:hi] for lo, hi in COL_CHUNKS]
+            sent, kept = [], []
+            for col in cols:
+                sent.append(partial_grad(col, h_other))
+            for col in cols:
+                kept.append(partial_grad(col, h_own))
+            d_proj, _, _ = lax.optimization_barrier((d_proj, sent, kept))
+            in_parts = [spread(a, b, 1) for a, b in zip(sent, kept)]
+            d_h = jnp.dot(d_proj[:, :PROJ], full_in, preferred_element_type=F32).astype(BF16)
             d_u_norm, g_norm = norm_pull(d_h)
             d_u = (d_out.astype(F32) + d_u_norm.astype(F32)).astype(BF16)
             g_conv = jnp.concatenate([g_ch[:5], g_bc[:5]], axis=1)
@@ -438,7 +611,7 @@
 
         u_rows, d_out = u_loc[0], g_loc[0]
         small_one, small_two = small_layer(0), small_layer(1)
-        in_one, out_one, in_two, out_two = gather_in_order([w_in[0], w_out[0], w_in[1], w_out[1]])
+        in_one, out_one, in_two, out_two = gather_weights(w_in.swapaxes(1, 2), w_out)
         hidden, saved_one = layer_forward(u_rows, small_one, in_one, out_one)
         out_rows, saved_two = layer_forward(hidden, small_two, in_two, out_two)
         d_hidden, out_parts_two, in_parts_two, smalls_two = layer_backward(d_out, saved_two, small_two, in_two, out_two)
@@ -446,12 +619,10 @@
 
         g_in = jnp.zeros((2, PROJ, w_in.shape[1]), F32)
         g_out = jnp.zeros((2,) + w_out.shape[1:], F32)
-        g_out = place(g_out, 1, out_parts_two, 0, g_out.shape[1])
-        for (lo, hi), parts in zip(COL_CHUNKS, in_parts_two):
-            g_in = place(g_in, 1, parts, lo, min(hi, PROJ) - lo)
-        g_out = place(g_out, 0, out_parts_one, 0, g_out.shape[1])
-        for (lo, hi), parts in zip(COL_CHUNKS, in_parts_one):
-            g_in = place(g_in, 0, parts, lo, min(hi, PROJ) - lo)
+        for layer, in_parts, out_part in ((1, in_parts_two, out_parts_two), (0, in_parts_one, out_parts_one)):
+            g_out = lax.dynamic_update_slice(g_out, out_part[None], (layer, 0, 0))
+            for (lo, hi), part in zip(COL_CHUNKS, in_parts):
+                g_in = lax.dynamic_update_slice(g_in, part[None, :min(hi, PROJ) - lo], (layer, lo, 0))
 
         def small_piece_rows(smalls):
             vals = []
@@ -467,7 +638,7 @@
         both = jnp.stack([small_piece_rows(smalls_one), small_piece_rows(smalls_two)], axis=1)
         for axis in ('fsdp', 'dp'):
             for k in (1, 2):
-                both = both + lax.ppermute(both, axis, [(i, i ^ k) for i in range(4)])
+                both = both + lax.ppermute(both, axis, swap(k))
         summed = lax.dynamic_index_in_dim(both, me_fsdp, 0, keepdims=False)
         outs, at = [], 0
         for width in widths:

time: 1410 us -> 1070 us (0.76)
  waiting for transfers between devices: 695 us -> 289 us
  Pallas kernels: 178 us -> 313 us
  local copies, waits for them, and re-layouts: 215 us -> 100 us
  other arithmetic: 32.1 us -> 108 us
  starting transfers between devices: 66 us -> 39.9 us
    all_gather x4 -> x8, waiting for transfers between devices: 310 us -> 5.63 us  [spread(): return lax.all_gather(total, 'dp', axis=0, tiled=True)]
    reduce_scatter x8 -> x0, waiting for transfers between devices: 144 us -> none  [spread(): piece = lax.psum_scatter(part, 'fsdp', scatter_dimension=0, tiled=True)]
    pallas_call x0 -> x1, Pallas kernels: none -> 140 us  [gather_weights(): pl.pallas_call(gather_kernel, in_specs=[hbm, hbm], out_specs=[hbm] * 4, o...]
    dynamic_update_slice x32 -> x6, local copies, waits for them, and re-layouts: 118 us -> 29.8 us  [per_device(): lax.dynamic_update_slice(g_in, part[None, :min(hi, PROJ) - lo], (layer, l...]
    add x4 -> x20, other arithmetic: 1.26 us -> 54.9 us  [the longest x8 34.4 us: spread(): pair = kept + got]
    ppermute x52 -> x44, waiting for transfers between devices: 238 us -> 283 us  [the longest x8 177 us: spread(): lax.ppermute(lax.dynamic_slice_in_dim(pair, (1 - chip_u) * size, size, ax...]
    ppermute x52 -> x44, starting transfers between devices: 65.6 us -> 38.5 us  [the longest x24 28.7 us: spread(): terms[k] = lax.ppermute(terms[k], 'dp', swap(k))]
    dot_general x8 -> x16, matrix products: 64.6 us -> 84.8 us  [partial_grad(): lax.dot_general(left, right, TN, preferred_element_type=F32) / batch_tot]
  transfers between devices with their start and end apart: 64 -> 52, of which waited for: 25 -> 28; matrix products, arithmetic and copies ran while one was open for 29% -> 26% of each run, Pallas kernels for 13% -> 6%
where the time goes in v2:
time: 1070 us; the launch traced here: 1060 us
  Pallas kernels  313 us (29%)
  waiting for transfers between devices  289 us (27%)
  matrix products  190 us (18%)
  other arithmetic  108 us (10%)
  local copies, waits for them, and re-layouts  100 us (9%)
  starting transfers between devices  39.9 us (4%)
  between operations  15.8 us (1%)
    ppermute x8, waiting for transfers between devices, spread(): lax.ppermute(lax.dynamic_slice_in_dim(pair, (1 - chip_u) * size, size, ax...  177 us
    pallas_call x1, Pallas kernels, gather_weights(): pl.pallas_call(gather_kernel, in_specs=[hbm, hbm], out_specs=[hbm] * 4, o...  140 us
    pallas_call x2, Pallas kernels, mixer_bwd(): pl.pallas_call(bwd_kernel, grid=(2, N_PAIRS), in_specs=[pl.BlockSpec((1,...  121 us
    ppermute x24, waiting for transfers between devices, spread(): terms[k] = lax.ppermute(terms[k], 'dp', swap(k))  96.6 us
    dot_general x16, matrix products, partial_grad(): lax.dot_general(left, right, TN, preferred_element_type=F32) / batch_tot  84.8 us
    pallas_call x2, Pallas kernels, mixer_fwd(): pl.pallas_call(fwd_kernel, grid=(N_PAIRS,), in_specs=[pl.BlockSpec((1, 8,...  51.8 us
    dot_general x2, matrix products, layer_backward(): jnp.dot(d_proj[:, :PROJ], full_in, preferred_element_type=F32).astype(BF16)  37.3 us
    add x8, other arithmetic, spread(): pair = kept + got  34.4 us
  transfers between devices with their start and end apart: 52, of which 28 were waited for; matrix products, arithmetic and copies ran while one was open for 26% of the time, Pallas kernels for 6%

profile of v2, /device:TPU:0, one launch (start us, length us, event | category | flops | bytes accessed | tf_op | source)
XLA Modules:
  0.0 1062.7 jit_solution(5309288593081786268)
XLA Ops:
  9.0 7.0 all-gather.1
  24.2 140.3 %gather_weights.1 = (bf16[6448,1536]{1,0:T(8,128)(2,1)}, bf16[3072,1536]{1,0:T(8,128)(2,1)S(1)}, bf16[6448,1536]{1,0:T(8,128)(2,1)}, bf16[3072,1536]{1,0:T(8,128)(2,1)}) custom-call(bf16[2,6448,384]{2,1,0:T(8,128)(2,1)} %bitcast.216, bf16[2,768,1536]{2,1,0:T(8,128)(2,1)S(1)} %copy-done), custom_call_target="tpu_custom_call" | custom-call | flops 1000000000 | bytes 100000000 | tf_op jit(solution)/shard_map/gather_weights/pallas_call | solution.py:481
  168.3 16.6 %convolution_convert_fusion.1.x_ref.z_ref.b_ref.c_ref = bf16[512,6448]{1,0:T(8,128)(2,1)} fusion(bf16[512,1536]{1,0:T(8,128)(2,1)S(1)} %fusion.14, bf16[6448,1536]{1,0:T(8,128)(2,1)} %get-tuple-element.77), kind=kOutput, calls=%fused_computation.1 | convolution fusion | flops 10145128448 | bytes 27983872 | tf_op jit(solution)/shard_map/dot_general | solution.py:516
  188.2 26.3 %mixer_fwd.2 = (f32[512,3072]{1,0:T(8,128)S(1)}, bf16[512,3072]{1,0:T(8,128)(2,1)S(1)}, f32[512,128]{1,0:T(8,128)S(1)}) custom-call(f32[24,8,512]{2,1,0:T(8,128)S(1)} %maximum_maximum_fusion.rows_ref, bf16[512,6448]{1,0:T(8,128)(2,1)} %convolution_convert_fusion.1.x_ref.z_ref.b_ref.c_ref, ...), custom_call_target="tpu_custom_call" | custom-call | flops 8000000000 | bytes 16000000 | tf_op jit(solution)/shard_map/mixer_fwd/pallas_call | solution.py:268
  222.6 17.6 %convolution_convert_fusion.x_ref.z_ref.b_ref.c_ref = bf16[512,6448]{1,0:T(8,128)(2,1)} fusion(bf16[512,1536]{1,0:T(8,128)(2,1)} %fusion.15, bf16[6448,1536]{1,0:T(8,128)(2,1)} %get-tuple-element.81), kind=kOutput, calls=%fused_computation | convolution fusion | flops 10145128448 | bytes 27983872 | tf_op jit(solution)/shard_map/dot_general | solution.py:516
  246.3 25.5 %mixer_fwd.3 = (f32[512,3072]{1,0:T(8,128)S(1)}, bf16[512,3072]{1,0:T(8,128)(2,1)S(1)}, f32[512,128]{1,0:T(8,128)S(1)}) custom-call(f32[24,8,512]{2,1,0:T(8,128)S(1)} %maximum_maximum_fusion.1.rows_ref, bf16[512,6448]{1,0:T(8,128)(2,1)} %convolution_convert_fusion.x_ref.z_ref.b_ref.c_ref, bf16[512,6448]{1,0:T(8,128)(2,1)} %convolution_convert_fusion.x_ref.z_ref.b_ref.c_ref, ...), custom_call_target="tpu_custom_call" | custom-call | flops 8000000000 | bytes 16000000 | tf_op jit(solution)/shard_map/mixer_fwd/pallas_call | solution.py:268
  285.4 60.6 %mixer_bwd.2 = (bf16[512,6528]{1,0:T(8,128)(2,1)}, f32[24,8,512]{2,1,0:T(8,128)S(1)}, f32[8,3072]{1,0:T(8,128)S(1)}, f32[8,256]{1,0:T(8,128)S(1)}) custom-call(f32[24,8,512]{2,1,0:T(8,128)S(1)} %maximum_maximum_fusion.1.rows_ref, bf16[512,6448]{1,0:T(8,128)(2,1)} %convolution_convert_fusion.x_ref.z_ref.b_ref.c_ref, ...), custom_call_target="tpu_custom_call" | custom-call | flops 16000000000 | bytes 40000000 | tf_op jit(solution)/shard_map/mixer_bwd/pallas_call | solution.py:296
  356.5 5.7 multiply_convert_fusion.11
  392.1 27.7 %collective-permute-done.5 = bf16[2176,384]{1,0:T(8,128)(2,1)} collective-permute-done((bf16[2176,384]{1,0:T(8,128)(2,1)}, bf16[2176,384]{1,0:T(8,128)(2,1)}, u32[]{:S(2)}, u32[]{:S(2)}) %collective-permute-start.5) | collective-permute-done | bytes 1671200 | tf_op jit(solution)/shard_map/ppermute | solution.py:573
  438.9 5.7 collective-permute-done.8
  448.6 18.5 %fusion.20 = (f32[1536]{0:T(1024)}, f32[512]{0:T(512)S(1)}, bf16[512,1536]{1,0:T(8,128)(2,1)S(1)}) fusion(bf16[512,1536]{1,0:T(8,128)(2,1)} %copy-done.29, f32[512]{0:T(512)S(1)} %copy-done.77, f32[1536]{0:T(1024)S(1)} %copy-done.69, bf16[6448,1536]{1,0:T(8,128)(2,1)} %get-tuple-element.81, bf16[512,6528]{1,0:T(8,128)(2,1)} %dynamic_update_slice.28), kind=kOutput, calls=%fused_computation.60 | convolution fusion | flops 10148902912 | bytes 29655040 | tf_op jit(solution)/shard_map/dot_general | solution.py:604
  483.7 10.3 convolution_convert_fusion.2.dn_ref
  500.1 8.9 collective-permute-done.13
  519.2 60.6 %mixer_bwd.3 = (bf16[512,6528]{1,0:T(8,128)(2,1)}, f32[24,8,512]{2,1,0:T(8,128)S(1)}, f32[8,3072]{1,0:T(8,128)S(1)}, f32[8,256]{1,0:T(8,128)S(1)}) custom-call(f32[24,8,512]{2,1,0:T(8,128)S(1)} %copy-done.4, bf16[512,6448]{1,0:T(8,128)(2,1)} %convolution_convert_fusion.1.x_ref.z_ref.b_ref.c_ref, ...), custom_call_target="tpu_custom_call" | custom-call | flops 16000000000 | bytes 40000000 | tf_op jit(solution)/shard_map/mixer_bwd/pallas_call | solution.py:296
  596.8 9.0 collective-permute-done.16
  605.9 8.7 collective-permute-done.18
  635.2 32.0 %collective-permute-done.20 = bf16[2176,384]{1,0:T(8,128)(2,1)} collective-permute-done((bf16[2176,384]{1,0:T(8,128)(2,1)}, bf16[2176,384]{1,0:T(8,128)(2,1)}, u32[]{:S(2)}, u32[]{:S(2)}) %collective-permute-start.20) | collective-permute-done | bytes 1671200 | tf_op jit(solution)/shard_map/ppermute | solution.py:573
  673.9 9.0 collective-permute-done.21
  682.9 7.5 collective-permute-done.23
  710.9 29.3 %collective-permute-done.25 = bf16[2176,384]{1,0:T(8,128)(2,1)} collective-permute-done((bf16[2176,384]{1,0:T(8,128)(2,1)}, bf16[2176,384]{1,0:T(8,128)(2,1)}, u32[]{:S(2)}, u32[]{:S(2)}) %collective-permute-start.25) | collective-permute-done | bytes 1671200 | tf_op jit(solution)/shard_map/ppermute | solution.py:573
  746.9 8.4 collective-permute-done.26
  774.4 30.8 %collective-permute-done.30 = bf16[2176,384]{1,0:T(8,128)(2,1)} collective-permute-done((bf16[2176,384]{1,0:T(8,128)(2,1)}, bf16[2176,384]{1,0:T(8,128)(2,1)}, u32[]{:S(2)}, u32[]{:S(2)}) %collective-permute-start.30) | collective-permute-done | bytes 1671200 | tf_op jit(solution)/shard_map/ppermute | solution.py:573
  829.4 18.8 %fusion.21 = (f32[1536]{0:T(1024)}, f32[512]{0:T(512)}, bf16[512,1536]{1,0:T(8,128)(2,1)}) fusion(bf16[1,512,1536]{2,1,0:T(8,128)(2,1)S(1)} %copy-done.19, f32[512]{0:T(512)S(1)} %copy-done.74, f32[1536]{0:T(1024)S(1)} %copy-done.67, bf16[6448,1536]{1,0:T(8,128)(2,1)} %get-tuple-element.77, bf16[512,6528]{1,0:T(8,128)(2,1)} %dynamic_update_slice.29), kind=kOutput, calls=%fused_computation.61 | convolution fusion | flops 10148902912 | bytes 29655040 | tf_op jit(solution)/shard_map/dot_general | solution.py:604
  849.0 22.2 %collective-permute-done.35 = bf16[768,1536]{1,0:T(8,128)(2,1)} collective-permute-done((bf16[768,1536]{1,0:T(8,128)(2,1)}, bf16[768,1536]{1,0:T(8,128)(2,1)}, u32[]{:S(2)}, u32[]{:S(2)}) %collective-permute-start.35) | collective-permute-done | bytes 2359328 | tf_op jit(solution)/shard_map/ppermute | solution.py:573
  890.3 7.3 collective-permute-done.38
  902.9 6.7 fusion.3
  921.0 10.2 fusion.34
  931.2 32.3 %collective-permute-done.40 = bf16[768,1536]{1,0:T(8,128)(2,1)} collective-permute-done((bf16[768,1536]{1,0:T(8,128)(2,1)}, bf16[768,1536]{1,0:T(8,128)(2,1)}, u32[]{:S(2)}, u32[]{:S(2)}) %collective-permute-start.40) | collective-permute-done | bytes 2359328 | tf_op jit(solution)/shard_map/ppermute | solution.py:573
  973.8 6.6 collective-permute-done.41
  980.4 8.7 collective-permute-done.43
  1011.8 10.6 dynamic_update_slice.30
  1047.3 8.4 pad_maximum_fusion
  (499 shorter events, 349.2 us)
Async XLA Ops:
  7.2 1004.6 %all-gather.11.cloned.1.call-start = ((), (), s32[]{:S(2)}) async-start(), calls=%async_computation | async-start | bytes 4177920 | tf_op jit(solution)/shard_map/all_gather | solution.py:582
  368.0 65.1 %collective-permute-start.9 = (bf16[2176,768]{1,0:T(8,128)(2,1)}, bf16[2176,768]{1,0:T(8,128)(2,1)}, u32[]{:S(2)}, u32[]{:S(2)}) collective-permute-start(bf16[2176,768]{1,0:T(8,128)(2,1)} %multiply_convert_fusion.10), channel_id=1, source_target_pairs={{0,1},{1,0},{2,3},{3,2},{4,5},{5,4},{6,7},{7,6},{8,9},{9,8},{10,11... | collective-permute-start | bytes 10027016 | tf_op jit(solution)/shard_map/ppermute | solution.py:569
  380.6 39.2 %collective-permute-start.5 = (bf16[2176,384]{1,0:T(8,128)(2,1)}, bf16[2176,384]{1,0:T(8,128)(2,1)}, u32[]{:S(2)}, u32[]{:S(2)}) collective-permute-start(bf16[2176,384]{1,0:T(8,128)(2,1)} %constant_dynamic-slice_fusion.11), channel_id=1, source_target_pairs={{0,2},{1,3},{2,0},{3,1},{4,6},{5,7},{6,4},{7,5},{8,10},{9,11},{10,... | collective-permute-start | bytes 5013512 | tf_op jit(solution)/shard_map/ppermute | solution.py:573
  386.5 107.5 %collective-permute-start.14 = (bf16[2176,768]{1,0:T(8,128)(2,1)}, bf16[2176,768]{1,0:T(8,128)(2,1)}, u32[]{:S(2)}, u32[]{:S(2)}) collective-permute-start(bf16[2176,768]{1,0:T(8,128)(2,1)} %multiply_convert_fusion.9), channel_id=1, source_target_pairs={{0,1},{1,0},{2,3},{3,2},{4,5},{5,4},{6,7},{7,6},{8,9},{9,8},{10,11... | collective-permute-start | bytes 10027016 | tf_op jit(solution)/shard_map/ppermute | solution.py:569
  424.6 19.9 %collective-permute-start.8 = (bf16[544,384]{1,0:T(8,128)(2,1)}, bf16[544,384]{1,0:T(8,128)(2,1)}, u32[]{:S(2)}, u32[]{:S(2)}) collective-permute-start(bf16[544,384]{1,0:T(8,128)(2,1)} %get-tuple-element.191), channel_id=1, source_target_pairs={{0,12},{4,8},{8,4},{12,0},{1,13},{5,9},{9,5},{13,1},{2,14},{6,10},... | collective-permute-start | bytes 1253384 | tf_op jit(solution)/shard_map/ppermute | solution.py:579
  438.3 37.5 %collective-permute-start.10 = (bf16[2176,384]{1,0:T(8,128)(2,1)}, bf16[2176,384]{1,0:T(8,128)(2,1)}, u32[]{:S(2)}, u32[]{:S(2)}) collective-permute-start(bf16[2176,384]{1,0:T(8,128)(2,1)} %constant_dynamic-slice_fusion.10), channel_id=1, source_target_pairs={{0,2},{1,3},{2,0},{3,1},{4,6},{5,7},{6,4},{7,5},{8,10},{9,11},{10,... | collective-permute-start | bytes 5013512 | tf_op jit(solution)/shard_map/ppermute | solution.py:573
  448.5 573.9 %all-gather.13.cloned.1.call-start = ((), (), s32[]{:S(2)}) async-start(), calls=%async_computation.1 | async-start | bytes 4177920 | tf_op jit(solution)/shard_map/all_gather | solution.py:582
  480.7 28.3 %collective-permute-start.13 = (bf16[544,384]{1,0:T(8,128)(2,1)}, bf16[544,384]{1,0:T(8,128)(2,1)}, u32[]{:S(2)}, u32[]{:S(2)}) collective-permute-start(bf16[544,384]{1,0:T(8,128)(2,1)} %get-tuple-element.188), channel_id=1, source_target_pairs={{0,12},{4,8},{8,4},{12,0},{1,13},{5,9},{9,5},{13,1},{2,14},{6,10},... | collective-permute-start | bytes 1253384 | tf_op jit(solution)/shard_map/ppermute | solution.py:579
  482.2 26.9 %collective-permute-start.12 = (bf16[544,384]{1,0:T(8,128)(2,1)}, bf16[544,384]{1,0:T(8,128)(2,1)}, u32[]{:S(2)}, u32[]{:S(2)}) collective-permute-start(bf16[544,384]{1,0:T(8,128)(2,1)} %get-tuple-element.189), channel_id=1, source_target_pairs={{0,8},{4,12},{8,0},{12,4},{1,9},{5,13},{9,1},{13,5},{2,10},{6,14},... | collective-permute-start | bytes 1253384 | tf_op jit(solution)/shard_map/ppermute | solution.py:579
  511.5 514.7 %all-gather.15.cloned.1.call-start = ((), (), s32[]{:S(2)}) async-start(), calls=%async_computation.2 | async-start | bytes 4177920 | tf_op jit(solution)/shard_map/all_gather | solution.py:582
  514.5 75.5 %collective-permute-start.15 = (bf16[2176,384]{1,0:T(8,128)(2,1)}, bf16[2176,384]{1,0:T(8,128)(2,1)}, u32[]{:S(2)}, u32[]{:S(2)}) collective-permute-start(bf16[2176,384]{1,0:T(8,128)(2,1)} %constant_dynamic-slice_fusion.9), channel_id=1, source_target_pairs={{0,2},{1,3},{2,0},{3,1},{4,6},{5,7},{6,4},{7,5},{8,10},{9,11},{10,... | collective-permute-start | bytes 5013512 | tf_op jit(solution)/shard_map/ppermute | solution.py:573
  590.1 33.6 %collective-permute-start.19 = (bf16[2176,768]{1,0:T(8,128)(2,1)}, bf16[2176,768]{1,0:T(8,128)(2,1)}, u32[]{:S(2)}, u32[]{:S(2)}) collective-permute-start(bf16[2176,768]{1,0:T(8,128)(2,1)} %multiply_convert_fusion.5), channel_id=1, source_target_pairs={{0,1},{1,0},{2,3},{3,2},{4,5},{5,4},{6,7},{7,6},{8,9},{9,8},{10,11... | collective-permute-start | bytes 10027016 | tf_op jit(solution)/shard_map/ppermute | solution.py:569
  594.0 20.5 %collective-permute-start.18 = (bf16[544,384]{1,0:T(8,128)(2,1)S(1)}, bf16[544,384]{1,0:T(8,128)(2,1)S(1)}, u32[]{:S(2)}, u32[]{:S(2)}) collective-permute-start(bf16[544,384]{1,0:T(8,128)(2,1)S(1)} %get-tuple-element.185), channel_id=1, source_target_pairs={{0,12},{4,8},{8,4},{12,0},{1,13},{5,9},{9,5},{13,1},{2,14},{6,10},... | collective-permute-start | bytes 1253384 | tf_op jit(solution)/shard_map/ppermute | solution.py:579
  595.5 20.4 %collective-permute-start.17 = (bf16[544,384]{1,0:T(8,128)(2,1)S(1)}, bf16[544,384]{1,0:T(8,128)(2,1)S(1)}, u32[]{:S(2)}, u32[]{:S(2)}) collective-permute-start(bf16[544,384]{1,0:T(8,128)(2,1)S(1)} %get-tuple-element.186), channel_id=1, source_target_pairs={{0,8},{4,12},{8,0},{12,4},{1,9},{5,13},{9,1},{13,5},{2,10},{6,14},... | collective-permute-start | bytes 1253384 | tf_op jit(solution)/shard_map/ppermute | solution.py:579
  618.1 412.0 %all-gather.17.cloned.1.call-start = ((), (), s32[]{:S(2)}) async-start(), calls=%async_computation.3 | async-start | bytes 4177920 | tf_op jit(solution)/shard_map/all_gather | solution.py:582
  629.1 38.1 %collective-permute-start.20 = (bf16[2176,384]{1,0:T(8,128)(2,1)}, bf16[2176,384]{1,0:T(8,128)(2,1)}, u32[]{:S(2)}, u32[]{:S(2)}) collective-permute-start(bf16[2176,384]{1,0:T(8,128)(2,1)} %constant_dynamic-slice_fusion.8), channel_id=1, source_target_pairs={{0,2},{1,3},{2,0},{3,1},{4,6},{5,7},{6,4},{7,5},{8,10},{9,11},{10,... | collective-permute-start | bytes 5013512 | tf_op jit(solution)/shard_map/ppermute | solution.py:573
  635.2 64.3 %collective-permute-start.24 = (bf16[2176,768]{1,0:T(8,128)(2,1)}, bf16[2176,768]{1,0:T(8,128)(2,1)}, u32[]{:S(2)}, u32[]{:S(2)}) collective-permute-start(bf16[2176,768]{1,0:T(8,128)(2,1)} %multiply_convert_fusion.4), channel_id=1, source_target_pairs={{0,1},{1,0},{2,3},{3,2},{4,5},{5,4},{6,7},{7,6},{8,9},{9,8},{10,11... | collective-permute-start | bytes 10027016 | tf_op jit(solution)/shard_map/ppermute | solution.py:569
  693.9 340.0 %all-gather.19.cloned.1.call-start = ((), (), s32[]{:S(2)}) async-start(), calls=%async_computation.4 | async-start | bytes 4177920 | tf_op jit(solution)/shard_map/all_gather | solution.py:582
  704.7 35.5 %collective-permute-start.25 = (bf16[2176,384]{1,0:T(8,128)(2,1)}, bf16[2176,384]{1,0:T(8,128)(2,1)}, u32[]{:S(2)}, u32[]{:S(2)}) collective-permute-start(bf16[2176,384]{1,0:T(8,128)(2,1)} %constant_dynamic-slice_fusion.7), channel_id=1, source_target_pairs={{0,2},{1,3},{2,0},{3,1},{4,6},{5,7},{6,4},{7,5},{8,10},{9,11},{10,... | collective-permute-start | bytes 5013512 | tf_op jit(solution)/shard_map/ppermute | solution.py:573
  710.8 58.1 %collective-permute-start.29 = (bf16[2176,768]{1,0:T(8,128)(2,1)}, bf16[2176,768]{1,0:T(8,128)(2,1)}, u32[]{:S(2)}, u32[]{:S(2)}) collective-permute-start(bf16[2176,768]{1,0:T(8,128)(2,1)} %multiply_convert_fusion.3), channel_id=1, source_target_pairs={{0,1},{1,0},{2,3},{3,2},{4,5},{5,4},{6,7},{7,6},{8,9},{9,8},{10,11... | collective-permute-start | bytes 10027016 | tf_op jit(solution)/shard_map/ppermute | solution.py:569
  746.9 70.4 %collective-permute-start.34 = (bf16[1536,1536]{1,0:T(8,128)(2,1)}, bf16[1536,1536]{1,0:T(8,128)(2,1)}, u32[]{:S(2)}, u32[]{:S(2)}) collective-permute-start(bf16[1536,1536]{1,0:T(8,128)(2,1)} %fusion.1), channel_id=1, source_target_pairs={{0,1},{1,0},{2,3},{3,2},{4,5},{5,4},{6,7},{7,6},{8,9},{9,8},{10,11... | collective-permute-start | bytes 14155784 | tf_op jit(solution)/shard_map/ppermute | solution.py:569
  763.1 274.7 %all-gather.21.cloned.1.call-start = ((), (), s32[]{:S(2)}) async-start(), calls=%async_computation.5 | async-start | bytes 4177920 | tf_op jit(solution)/shard_map/all_gather | solution.py:582
  774.3 30.9 %collective-permute-start.30 = (bf16[2176,384]{1,0:T(8,128)(2,1)}, bf16[2176,384]{1,0:T(8,128)(2,1)}, u32[]{:S(2)}, u32[]{:S(2)}) collective-permute-start(bf16[2176,384]{1,0:T(8,128)(2,1)} %constant_dynamic-slice_fusion.6), channel_id=1, source_target_pairs={{0,2},{1,3},{2,0},{3,1},{4,6},{5,7},{6,4},{7,5},{8,10},{9,11},{10,... | collective-permute-start | bytes 5013512 | tf_op jit(solution)/shard_map/ppermute | solution.py:573
  774.4 135.2 %collective-permute-start.39 = (bf16[1536,1536]{1,0:T(8,128)(2,1)}, bf16[1536,1536]{1,0:T(8,128)(2,1)}, u32[]{:S(2)}, u32[]{:S(2)}) collective-permute-start(bf16[1536,1536]{1,0:T(8,128)(2,1)} %fusion), channel_id=1, source_target_pairs={{0,1},{1,0},{2,3},{3,2},{4,5},{5,4},{6,7},{7,6},{8,9},{9,8},{10,11... | collective-permute-start | bytes 14155784 | tf_op jit(solution)/shard_map/ppermute | solution.py:569
  826.1 45.1 %collective-permute-start.35 = (bf16[768,1536]{1,0:T(8,128)(2,1)}, bf16[768,1536]{1,0:T(8,128)(2,1)}, u32[]{:S(2)}, u32[]{:S(2)}) collective-permute-start(bf16[768,1536]{1,0:T(8,128)(2,1)} %constant_dynamic-slice_fusion.3), channel_id=1, source_target_pairs={{0,2},{1,3},{2,0},{3,1},{4,6},{5,7},{6,4},{7,5},{8,10},{9,11},{10,... | collective-permute-start | bytes 7077896 | tf_op jit(solution)/shard_map/ppermute | solution.py:573
  828.9 212.8 %all-gather.23.cloned.1.call-start = ((), (), s32[]{:S(2)}) async-start(), calls=%async_computation.6 | async-start | bytes 5898240 | tf_op jit(solution)/shard_map/all_gather | solution.py:582
  875.9 21.7 %collective-permute-start.38 = (bf16[192,1536]{1,0:T(8,128)(2,1)}, bf16[192,1536]{1,0:T(8,128)(2,1)}, u32[]{:S(2)}, u32[]{:S(2)}) collective-permute-start(bf16[192,1536]{1,0:T(8,128)(2,1)} %get-tuple-element.170), channel_id=1, source_target_pairs={{0,12},{4,8},{8,4},{12,0},{1,13},{5,9},{9,5},{13,1},{2,14},{6,10},... | collective-permute-start | bytes 1769480 | tf_op jit(solution)/shard_map/ppermute | solution.py:579
  901.3 146.0 %all-gather.25.cloned.1.call-start = ((), (), s32[]{:S(2)}) async-start(), calls=%async_computation.7 | async-start | bytes 5898240 | tf_op jit(solution)/shard_map/all_gather | solution.py:582
  918.5 45.0 %collective-permute-start.40 = (bf16[768,1536]{1,0:T(8,128)(2,1)}, bf16[768,1536]{1,0:T(8,128)(2,1)}, u32[]{:S(2)}, u32[]{:S(2)}) collective-permute-start(bf16[768,1536]{1,0:T(8,128)(2,1)} %constant_dynamic-slice_fusion), channel_id=1, source_target_pairs={{0,2},{1,3},{2,0},{3,1},{4,6},{5,7},{6,4},{7,5},{8,10},{9,11},{10,... | collective-permute-start | bytes 7077896 | tf_op jit(solution)/shard_map/ppermute | solution.py:573
  921.0 50.4 %collective-permute-start = (f32[4,2,5348]{2,0,1:T(4,128)}, f32[4,2,5348]{2,0,1:T(4,128)S(1)}, u32[]{:S(2)}, u32[]{:S(2)}) collective-permute-start(f32[4,2,5348]{2,0,1:T(4,128)} %pad_maximum_fusion.17), channel_id=1, source_target_pairs={{0,1},{1,0},{2,3},{3,2},{4,5},{5,4},{6,7},{7,6},{8,9},{9,8},{10,11... | collective-permute-start | bytes 513416 | tf_op jit(solution)/shard_map/ppermute | solution.py:641
  968.2 20.9 %collective-permute-start.43 = (bf16[192,1536]{1,0:T(8,128)(2,1)}, bf16[192,1536]{1,0:T(8,128)(2,1)}, u32[]{:S(2)}, u32[]{:S(2)}) collective-permute-start(bf16[192,1536]{1,0:T(8,128)(2,1)} %get-tuple-element.173), channel_id=1, source_target_pairs={{0,12},{4,8},{8,4},{12,0},{1,13},{5,9},{9,5},{13,1},{2,14},{6,10},... | collective-permute-start | bytes 1769480 | tf_op jit(solution)/shard_map/ppermute | solution.py:579
  972.1 20.0 %collective-permute-start.1 = (f32[4,2,5348]{2,0,1:T(4,128)}, f32[4,2,5348]{2,0,1:T(4,128)}, u32[]{:S(2)}, u32[]{:S(2)}) collective-permute-start(f32[4,2,5348]{2,0,1:T(4,128)} %fusion.122), channel_id=1, source_target_pairs={{0,2},{1,3},{2,0},{3,1},{4,6},{5,7},{6,4},{7,5},{8,10},{9,11},{10,... | collective-permute-start | bytes 513416 | tf_op jit(solution)/shard_map/ppermute | solution.py:641
  (125 other events, 3201.8 us)
Sparse Core Ops, SparseCore 0:
  448.6 50.1 all-gather.10
  511.7 40.8 all-gather.12
  618.2 40.8 all-gather.14
  694.1 39.9 all-gather.16
  763.3 41.9 all-gather.18
  829.0 43.7 all-gather.20
  901.4 52.2 all-gather.22
  992.2 55.0 all-gather.24

commit v3 on v2

--- a/solution.py
+++ b/solution.py
@@ -326,12 +326,11 @@
 
 
 IN_PART = 800
-OUT_PART = 192
-UNITS = ((0, 0, IN_PART), (0, 4 * IN_PART, IN_PART), (1, 0, OUT_PART))
+UNITS = ((0, IN_PART), (4 * IN_PART, IN_PART))
 N_UNITS = 2 * len(UNITS)
 
 
-def gather_kernel(win_ref, wout_ref, in_a, out_a, in_b, out_b, buf_in, buf_out, sends, recvs, tails, tailr, loads, stores):
+def gather_kernel(win_ref, in_a, in_b, buf_in, sends, recvs, tails, tailr, loads, stores):
     i, d = lax.axis_index('fsdp'), lax.axis_index('dp')
     x, c, z, y = i // 2, i % 2, d // 2, d % 2
     chip_x, core = 2 * (1 - x) + c, 2 * x + (1 - c)
@@ -344,21 +343,17 @@
         pl.semaphore_signal(barrier, inc=1, device_id=device, device_id_type=pl.DeviceIdType.MESH)
     pl.semaphore_wait(barrier, 4)
 
-    fulls = ((in_a, out_a), (in_b, out_b))
-    pieces, bufs = (win_ref, wout_ref), (buf_in, buf_out)
+    fulls = (in_a, in_b)
+    units = len(UNITS)
 
     def source(u, row, size):
-        layer, (kind, _, _) = u // 3, UNITS[u % 3]
-        return pieces[kind].at[layer, pl.ds(row, size), :]
+        return win_ref.at[u // units, pl.ds(row, size), :]
 
     def place(u, piece, row, size):
-        layer, (kind, _, _) = u // 3, UNITS[u % 3]
-        if kind == 0:
-            return fulls[layer][0].at[pl.ds(row, size), pl.ds(pl.multiple_of(piece * 384, 128), 384)]
-        return fulls[layer][1].at[pl.ds(pl.multiple_of(piece * 768 + row, 16), size), :]
+        return fulls[u // units].at[pl.ds(row, size), pl.ds(pl.multiple_of(piece * 384, 128), 384)]
 
     def span(u, q):
-        _, first, size = UNITS[u % 3]
+        first, size = UNITS[u % units]
         return pl.multiple_of(first + q * size, 16), size
 
     def copy(u, slot, src, dst, device):
@@ -376,7 +371,7 @@
         started.append(op)
 
     def tail_copy(layer, slot, src, device):
-        dst = fulls[layer][0].at[pl.ds(8 * IN_PART, N_HEADS), pl.ds(pl.multiple_of((i if slot < 2 else chip_x) * 384, 128), 384)]
+        dst = fulls[layer].at[pl.ds(8 * IN_PART, N_HEADS), pl.ds(pl.multiple_of((i if slot < 2 else chip_x) * 384, 128), 384)]
         return pltpu.make_async_remote_copy(
             src_ref=src, dst_ref=dst, send_sem=tails.at[layer, slot], recv_sem=tailr.at[layer, slot],
             device_id=device, device_id_type=pl.DeviceIdType.MESH)
@@ -392,22 +387,17 @@
             op.start()
             tails_own.append(op)
     for u in range(N_UNITS):
-        _, first, size = UNITS[u % 3]
+        first, size = UNITS[u % units]
         go(copy(u, 5, source(u, first, 4 * size), place(u, i, first, 4 * size), to_core))
 
-    local_in = [pltpu.make_async_copy(pieces[kind].at[layer], bufs[kind].at[layer], loads.at[layer, kind])
-                for layer in range(2) for kind in range(2)]
+    local_in = [pltpu.make_async_copy(win_ref.at[layer], buf_in.at[layer], loads.at[layer]) for layer in range(2)]
     for op in local_in:
         op.start()
     local_out = []
-    for n, op in enumerate(local_in):
-        layer, kind = n // 2, n % 2
+    for layer, op in enumerate(local_in):
         op.wait()
-        if kind == 0:
-            dst = fulls[layer][0].at[:, pl.ds(pl.multiple_of(i * 384, 128), 384)]
-        else:
-            dst = fulls[layer][1].at[pl.ds(pl.multiple_of(i * 768, 16), 768), :]
-        out = pltpu.make_async_copy(bufs[kind].at[layer], dst, stores.at[layer, kind])
+        dst = fulls[layer].at[:, pl.ds(pl.multiple_of(i * 384, 128), 384)]
+        out = pltpu.make_async_copy(buf_in.at[layer], dst, stores.at[layer])
         out.start()
         local_out.append(out)
 
@@ -422,7 +412,7 @@
         go(forward(u, 6, chip_x, row, size, to_core))
 
     def stage_two(u):
-        half = UNITS[u % 3][2] // 2
+        half = UNITS[u % units][1] // 2
         row, size = span(u, near_y)
         got(u, 1, chip_x, row, size)
         go(forward(u, 3, chip_x, row, half, to_z))
@@ -433,7 +423,7 @@
         go(forward(u, 8, chip_x, row, size, to_core))
 
     def stage_three(u):
-        half = UNITS[u % 3][2] // 2
+        half = UNITS[u % units][1] // 2
         row, _ = span(u, 2 * (1 - z) + (1 - y))
         got(u, 3, chip_x, row, half)
         go(forward(u, 9, chip_x, row, half, to_core))
@@ -449,7 +439,7 @@
             stage_three(t - 2)
 
     for layer in range(2):
-        tail_at = fulls[layer][0].at[pl.ds(8 * IN_PART, N_HEADS), pl.ds(pl.multiple_of(chip_x * 384, 128), 384)]
+        tail_at = fulls[layer].at[pl.ds(8 * IN_PART, N_HEADS), pl.ds(pl.multiple_of(chip_x * 384, 128), 384)]
         tail_copy(layer, 0, win_ref.at[layer, pl.ds(8 * IN_PART, N_HEADS), :], to_x).wait_recv()
         op = tail_copy(layer, 2, tail_at, to_core)
         op.start()
@@ -457,7 +447,7 @@
 
     diag, other_core_x = 2 * (1 - z) + (1 - y), 2 * (1 - x) + (1 - c)
     for u in range(N_UNITS):
-        _, first, size = UNITS[u % 3]
+        first, size = UNITS[u % units]
         half = size // 2
         got(u, 5, core, first, 4 * size)
         for slot, q in ((6, d), (7, near_y), (8, near_z)):
@@ -475,24 +465,23 @@
         op.wait()
 
 
-def gather_weights(w_in_t, w_out):
-    full = [jax.ShapeDtypeStruct((PROJ, D_MODEL), BF16), jax.ShapeDtypeStruct((D_INNER, D_MODEL), BF16)]
+def gather_w_in(w_in_t):
     hbm = pl.BlockSpec(memory_space=pltpu.HBM)
     return pl.pallas_call(
         gather_kernel,
-        in_specs=[hbm, hbm],
-        out_specs=[hbm] * 4,
-        out_shape=full + full,
+        in_specs=[hbm],
+        out_specs=[hbm] * 2,
+        out_shape=[jax.ShapeDtypeStruct((PROJ, D_MODEL), BF16)] * 2,
         scratch_shapes=[
-            pltpu.VMEM(w_in_t.shape, BF16), pltpu.VMEM(w_out.shape, BF16),
+            pltpu.VMEM(w_in_t.shape, BF16),
             pltpu.SemaphoreType.DMA((N_UNITS, 11)), pltpu.SemaphoreType.DMA((N_UNITS, 11)),
             pltpu.SemaphoreType.DMA((2, 3)), pltpu.SemaphoreType.DMA((2, 3)),
-            pltpu.SemaphoreType.DMA((2, 2)), pltpu.SemaphoreType.DMA((2, 2)),
+            pltpu.SemaphoreType.DMA((2,)), pltpu.SemaphoreType.DMA((2,)),
         ],
         compiler_params=pltpu.CompilerParams(collective_id=0, has_side_effects=True, vmem_limit_bytes=40 * 2 ** 20),
         cost_estimate=pl.CostEstimate(flops=10 ** 9, bytes_accessed=10 ** 8, transcendentals=0),
-        name="gather_weights",
-    )(w_in_t, w_out)
+        name="gather_w_in",
+    )(w_in_t)
 
 
 def pre_norm(u_rows, norm_w):
@@ -538,7 +527,7 @@
         widths = [piece.shape[1] for piece in small_pieces]
         packed = jnp.concatenate([piece.astype(F32) for piece in small_pieces], axis=1)
         gathered = lax.all_gather(packed, 'fsdp', axis=0)
-        w_in, w_out, gathered = lax.optimization_barrier((w_in, w_out, gathered))
+        w_in, gathered = lax.optimization_barrier((w_in, gathered))
 
         def small_layer(layer):
             vals, at = [], 0
@@ -611,7 +600,9 @@
 
         u_rows, d_out = u_loc[0], g_loc[0]
         small_one, small_two = small_layer(0), small_layer(1)
-        in_one, out_one, in_two, out_two = gather_weights(w_in.swapaxes(1, 2), w_out)
+        out_one = lax.all_gather(w_out[0], 'fsdp', axis=0, tiled=True)
+        out_two = lax.all_gather(w_out[1], 'fsdp', axis=0, tiled=True)
+        in_one, in_two = gather_w_in(w_in.swapaxes(1, 2))
         hidden, saved_one = layer_forward(u_rows, small_one, in_one, out_one)
         out_rows, saved_two = layer_forward(hidden, small_two, in_two, out_two)
         d_hidden, out_parts_two, in_parts_two, smalls_two = layer_backward(d_out, saved_two, small_two, in_two, out_two)

time: 1070 us -> 1080 us (level)
    unnamed x211 -> x173, local copies, waits for them, and re-layouts: 27.9 us -> 28.8 us
  transfers between devices with their start and end apart: 52 -> 54, of which waited for: 28 -> 27; matrix products, arithmetic and copies ran while one was open for 26% -> 32% of each run, Pallas kernels for 6% -> 23%
where the time goes in v3:
time: 1080 us; the launch traced here: 1070 us
  Pallas kernels  307 us (28%)
  waiting for transfers between devices  290 us (27%)
  matrix products  196 us (18%)
  other arithmetic  113 us (10%)
  local copies, waits for them, and re-layouts  102 us (9%)
  starting transfers between devices  39.5 us (4%)
  between operations  15.7 us (1%)
    ppermute x8, waiting for transfers between devices, spread(): lax.ppermute(lax.dynamic_slice_in_dim(pair, (1 - chip_u) * size, size, ax...  182 us
    pallas_call x1, Pallas kernels, gather_w_in(): pl.pallas_call(gather_kernel, in_specs=[hbm], out_specs=[hbm] * 2, out_sh...  135 us
    pallas_call x2, Pallas kernels, mixer_bwd(): pl.pallas_call(bwd_kernel, grid=(2, N_PAIRS), in_specs=[pl.BlockSpec((1,...  121 us
    ppermute x24, waiting for transfers between devices, spread(): terms[k] = lax.ppermute(terms[k], 'dp', swap(k))  91.7 us
    dot_general x16, matrix products, partial_grad(): lax.dot_general(left, right, TN, preferred_element_type=F32) / batch_tot  84.4 us
    pallas_call x2, Pallas kernels, mixer_fwd(): pl.pallas_call(fwd_kernel, grid=(N_PAIRS,), in_specs=[pl.BlockSpec((1, 8,...  50.8 us
    add x8, other arithmetic, spread(): pair = kept + got  41.7 us
    dot_general x2, matrix products, layer_backward(): jnp.dot(d_proj[:, :PROJ], full_in, preferred_element_type=F32).astype(BF16)  36.1 us
  transfers between devices with their start and end apart: 54, of which 27 were waited for; matrix products, arithmetic and copies ran while one was open for 32% of the time, Pallas kernels for 23%

profile of v3, /device:TPU:0, one launch (start us, length us, event | category | flops | bytes accessed | tf_op | source)
XLA Modules:
  0.0 1070.4 jit_solution(17923160107216113218)
XLA Ops:
  28.4 135.2 %gather_w_in.1 = (bf16[6448,1536]{1,0:T(8,128)(2,1)}, bf16[6448,1536]{1,0:T(8,128)(2,1)}) custom-call(bf16[2,6448,384]{2,1,0:T(8,128)(2,1)S(1)} %bitcast.227), custom_call_target="tpu_custom_call" | custom-call | flops 1000000000 | bytes 100000000 | tf_op jit(solution)/shard_map/gather_w_in/pallas_call | solution.py:470
  164.5 17.2 %convolution_convert_fusion.1.x_ref.z_ref.b_ref.c_ref = bf16[512,6448]{1,0:T(8,128)(2,1)} fusion(bf16[512,1536]{1,0:T(8,128)(2,1)S(1)} %fusion.32, bf16[6448,1536]{1,0:T(8,128)(2,1)} %get-tuple-element.73), kind=kOutput, calls=%fused_computation.1 | convolution fusion | flops 10145128448 | bytes 27983872 | tf_op jit(solution)/shard_map/dot_general | solution.py:505
  186.5 25.4 %mixer_fwd.2 = (f32[512,3072]{1,0:T(8,128)S(1)}, bf16[512,3072]{1,0:T(8,128)(2,1)S(1)}, f32[512,128]{1,0:T(8,128)S(1)}) custom-call(f32[24,8,512]{2,1,0:T(8,128)S(1)} %maximum_maximum_fusion.rows_ref, bf16[512,6448]{1,0:T(8,128)(2,1)} %convolution_convert_fusion.1.x_ref.z_ref.b_ref.c_ref, ...), custom_call_target="tpu_custom_call" | custom-call | flops 8000000000 | bytes 16000000 | tf_op jit(solution)/shard_map/mixer_fwd/pallas_call | solution.py:268
  216.0 9.4 fusion.40
  228.1 17.5 %convolution_convert_fusion.x_ref.z_ref.b_ref.c_ref = bf16[512,6448]{1,0:T(8,128)(2,1)} fusion(bf16[512,1536]{1,0:T(8,128)(2,1)} %fusion.33, bf16[6448,1536]{1,0:T(8,128)(2,1)} %get-tuple-element.76), kind=kOutput, calls=%fused_computation | convolution fusion | flops 10145128448 | bytes 27983872 | tf_op jit(solution)/shard_map/dot_general | solution.py:505
  252.5 25.4 %mixer_fwd.3 = (f32[512,3072]{1,0:T(8,128)S(1)}, bf16[512,3072]{1,0:T(8,128)(2,1)S(1)}, f32[512,128]{1,0:T(8,128)S(1)}) custom-call(f32[24,8,512]{2,1,0:T(8,128)S(1)} %maximum_maximum_fusion.1.rows_ref, bf16[512,6448]{1,0:T(8,128)(2,1)} %convolution_convert_fusion.x_ref.z_ref.b_ref.c_ref, bf16[512,6448]{1,0:T(8,128)(2,1)} %convolution_convert_fusion.x_ref.z_ref.b_ref.c_ref, ...), custom_call_target="tpu_custom_call" | custom-call | flops 8000000000 | bytes 16000000 | tf_op jit(solution)/shard_map/mixer_fwd/pallas_call | solution.py:268
  287.6 9.0 fusion.19.dn_ref
  299.4 60.2 %mixer_bwd.2 = (bf16[512,6528]{1,0:T(8,128)(2,1)}, f32[24,8,512]{2,1,0:T(8,128)S(1)}, f32[8,3072]{1,0:T(8,128)S(1)}, f32[8,256]{1,0:T(8,128)S(1)}) custom-call(f32[24,8,512]{2,1,0:T(8,128)S(1)} %maximum_maximum_fusion.1.rows_ref, bf16[512,6448]{1,0:T(8,128)(2,1)} %convolution_convert_fusion.x_ref.z_ref.b_ref.c_ref, ...), custom_call_target="tpu_custom_call" | custom-call | flops 16000000000 | bytes 40000000 | tf_op jit(solution)/shard_map/mixer_bwd/pallas_call | solution.py:296
  400.2 27.7 %collective-permute-done.5 = bf16[2176,384]{1,0:T(8,128)(2,1)} collective-permute-done((bf16[2176,384]{1,0:T(8,128)(2,1)S(1)}, bf16[2176,384]{1,0:T(8,128)(2,1)}, u32[]{:S(2)}, u32[]{:S(2)}) %collective-permute-start.5) | collective-permute-done | bytes 1671200 | tf_op jit(solution)/shard_map/ppermute | solution.py:562
  454.7 18.0 %fusion.38 = (f32[1536]{0:T(1024)S(1)}, f32[512]{0:T(512)S(1)}, bf16[512,1536]{1,0:T(8,128)(2,1)S(1)}) fusion(bf16[512,1536]{1,0:T(8,128)(2,1)} %copy-done.31, f32[512]{0:T(512)S(1)} %copy-done.67, f32[1536]{0:T(1024)S(1)} %copy-done.61, bf16[6448,1536]{1,0:T(8,128)(2,1)} %get-tuple-element.76, bf16[512,6528]{1,0:T(8,128)(2,1)} %dynamic_update_slice.28), kind=kOutput, calls=%fused_computation.68 | convolution fusion | flops 10148902912 | bytes 29655040 | tf_op jit(solution)/shard_map/dot_general | solution.py:593
  479.1 8.5 collective-permute-done.10
  494.7 10.3 fusion.16.dn_ref
  524.2 60.8 %mixer_bwd.3 = (bf16[512,6528]{1,0:T(8,128)(2,1)}, f32[24,8,512]{2,1,0:T(8,128)S(1)}, f32[8,3072]{1,0:T(8,128)S(1)}, f32[8,256]{1,0:T(8,128)S(1)}) custom-call(f32[24,8,512]{2,1,0:T(8,128)S(1)} %copy-done.4, bf16[512,6448]{1,0:T(8,128)(2,1)} %convolution_convert_fusion.1.x_ref.z_ref.b_ref.c_ref, ...), custom_call_target="tpu_custom_call" | custom-call | flops 16000000000 | bytes 40000000 | tf_op jit(solution)/shard_map/mixer_bwd/pallas_call | solution.py:296
  600.7 9.3 collective-permute-done.16
  610.1 8.5 collective-permute-done.18
  638.8 31.1 %collective-permute-done.20 = bf16[2176,384]{1,0:T(8,128)(2,1)} collective-permute-done((bf16[2176,384]{1,0:T(8,128)(2,1)S(1)}, bf16[2176,384]{1,0:T(8,128)(2,1)}, u32[]{:S(2)}, u32[]{:S(2)}) %collective-permute-start.20) | collective-permute-done | bytes 1671200 | tf_op jit(solution)/shard_map/ppermute | solution.py:562
  676.7 9.3 collective-permute-done.21
  686.0 7.6 collective-permute-done.23
  713.5 28.8 %collective-permute-done.25 = bf16[2176,384]{1,0:T(8,128)(2,1)} collective-permute-done((bf16[2176,384]{1,0:T(8,128)(2,1)S(1)}, bf16[2176,384]{1,0:T(8,128)(2,1)}, u32[]{:S(2)}, u32[]{:S(2)}) %collective-permute-start.25) | collective-permute-done | bytes 1671200 | tf_op jit(solution)/shard_map/ppermute | solution.py:562
  749.1 9.0 collective-permute-done.26
  777.9 30.2 %collective-permute-done.30 = bf16[2176,384]{1,0:T(8,128)(2,1)} collective-permute-done((bf16[2176,384]{1,0:T(8,128)(2,1)S(1)}, bf16[2176,384]{1,0:T(8,128)(2,1)}, u32[]{:S(2)}, u32[]{:S(2)}) %collective-permute-start.30) | collective-permute-done | bytes 1671200 | tf_op jit(solution)/shard_map/ppermute | solution.py:562
  821.8 7.3 add.483
  835.8 18.1 %fusion.39 = (f32[1536]{0:T(1024)S(1)}, f32[512]{0:T(512)S(1)}, bf16[512,1536]{1,0:T(8,128)(2,1)}) fusion(bf16[1,512,1536]{2,1,0:T(8,128)(2,1)S(1)} %copy-done.23, f32[512]{0:T(512)S(1)} %copy-done.65, f32[1536]{0:T(1024)S(1)} %copy-done.59, bf16[6448,1536]{1,0:T(8,128)(2,1)} %get-tuple-element.73, bf16[512,6528]{1,0:T(8,128)(2,1)} %dynamic_update_slice.29), kind=kOutput, calls=%fused_computation.69 | convolution fusion | flops 10148902912 | bytes 29655040 | tf_op jit(solution)/shard_map/dot_general | solution.py:593
  854.3 23.8 %collective-permute-done.35 = bf16[768,1536]{1,0:T(8,128)(2,1)} collective-permute-done((bf16[768,1536]{1,0:T(8,128)(2,1)}, bf16[768,1536]{1,0:T(8,128)(2,1)}, u32[]{:S(2)}, u32[]{:S(2)}) %collective-permute-start.35) | collective-permute-done | bytes 2359328 | tf_op jit(solution)/shard_map/ppermute | solution.py:562
  888.1 8.7 collective-permute-done.36
  896.8 7.3 collective-permute-done.38
  916.2 7.3 add.494
  929.2 10.7 %fusion.56 = bf16[1,512,1536]{2,1,0:T(8,128)(2,1)} fusion(bf16[512,3072]{1,0:T(8,128)(2,1)S(1)} %copy-done.2, bf16[1,3072,1536]{2,1,0:T(8,128)(2,1)} %all-gather.33.cloned.1.call-done, bf16[512,1536]{1,0:T(8,128)(2,1)} %copy-done.31), kind=kOutput, calls=%fused_computation.80 | convolution fusion | flops 4834197504 | bytes 15728640 | tf_op jit(solution)/shard_map/dot_general | solution.py:508
  940.0 31.5 %collective-permute-done.40 = bf16[768,1536]{1,0:T(8,128)(2,1)} collective-permute-done((bf16[768,1536]{1,0:T(8,128)(2,1)}, bf16[768,1536]{1,0:T(8,128)(2,1)}, u32[]{:S(2)}, u32[]{:S(2)}) %collective-permute-start.40) | collective-permute-done | bytes 2359328 | tf_op jit(solution)/shard_map/ppermute | solution.py:562
  988.1 9.1 collective-permute-done.43
  1018.9 10.6 dynamic_update_slice.30
  1055.0 8.4 pad_maximum_fusion
  (466 shorter events, 353.5 us)
Async XLA Ops:
  7.2 208.8 %all-gather.31.cloned.1.call-start = ((), (), s32[]{:S(2)}) async-start(), calls=%async_computation.8 | async-start | bytes 11796480 | tf_op jit(solution)/shard_map/all_gather | solution.py:603
  12.2 275.4 %all-gather.33.cloned.1.call-start = ((), (), s32[]{:S(2)}) async-start(), calls=%async_computation.9 | async-start | bytes 11796480 | tf_op jit(solution)/shard_map/all_gather | solution.py:604
  12.9 1006.0 %all-gather.15.cloned.1.call-start = ((), (), s32[]{:S(2)}) async-start(), calls=%async_computation | async-start | bytes 4177920 | tf_op jit(solution)/shard_map/all_gather | solution.py:571
  377.9 61.7 %collective-permute-start.9 = (bf16[2176,768]{1,0:T(8,128)(2,1)}, bf16[2176,768]{1,0:T(8,128)(2,1)}, u32[]{:S(2)}, u32[]{:S(2)}) collective-permute-start(bf16[2176,768]{1,0:T(8,128)(2,1)} %multiply_convert_fusion.10), channel_id=1, source_target_pairs={{0,1},{1,0},{2,3},{3,2},{4,5},{5,4},{6,7},{7,6},{8,9},{9,8},{10,11... | collective-permute-start | bytes 10027016 | tf_op jit(solution)/shard_map/ppermute | solution.py:558
  389.0 38.9 %collective-permute-start.5 = (bf16[2176,384]{1,0:T(8,128)(2,1)S(1)}, bf16[2176,384]{1,0:T(8,128)(2,1)}, u32[]{:S(2)}, u32[]{:S(2)}) collective-permute-start(bf16[2176,384]{1,0:T(8,128)(2,1)S(1)} %constant_dynamic-slice_fusion.11), channel_id=1, source_target_pairs={{0,2},{1,3},{2,0},{3,1},{4,6},{5,7},{6,4},{7,5},{8,10},{9,11},{10,... | collective-permute-start | bytes 5013512 | tf_op jit(solution)/shard_map/ppermute | solution.py:562
  439.6 65.3 %collective-permute-start.14 = (bf16[2176,768]{1,0:T(8,128)(2,1)}, bf16[2176,768]{1,0:T(8,128)(2,1)}, u32[]{:S(2)}, u32[]{:S(2)}) collective-permute-start(bf16[2176,768]{1,0:T(8,128)(2,1)} %multiply_convert_fusion.9), channel_id=1, source_target_pairs={{0,1},{1,0},{2,3},{3,2},{4,5},{5,4},{6,7},{7,6},{8,9},{9,8},{10,11... | collective-permute-start | bytes 10027016 | tf_op jit(solution)/shard_map/ppermute | solution.py:558
  448.4 39.2 %collective-permute-start.10 = (bf16[2176,384]{1,0:T(8,128)(2,1)}, bf16[2176,384]{1,0:T(8,128)(2,1)}, u32[]{:S(2)}, u32[]{:S(2)}) collective-permute-start(bf16[2176,384]{1,0:T(8,128)(2,1)} %constant_dynamic-slice_fusion.10), channel_id=1, source_target_pairs={{0,2},{1,3},{2,0},{3,1},{4,6},{5,7},{6,4},{7,5},{8,10},{9,11},{10,... | collective-permute-start | bytes 5013512 | tf_op jit(solution)/shard_map/ppermute | solution.py:562
  454.6 574.9 %all-gather.17.cloned.1.call-start = ((), (), s32[]{:S(2)}) async-start(), calls=%async_computation.1 | async-start | bytes 4177920 | tf_op jit(solution)/shard_map/all_gather | solution.py:571
  491.8 23.4 %collective-permute-start.13 = (bf16[544,384]{1,0:T(8,128)(2,1)}, bf16[544,384]{1,0:T(8,128)(2,1)}, u32[]{:S(2)}, u32[]{:S(2)}) collective-permute-start(bf16[544,384]{1,0:T(8,128)(2,1)} %get-tuple-element.184), channel_id=1, source_target_pairs={{0,12},{4,8},{8,4},{12,0},{1,13},{5,9},{9,5},{13,1},{2,14},{6,10},... | collective-permute-start | bytes 1253384 | tf_op jit(solution)/shard_map/ppermute | solution.py:568
  493.2 21.9 %collective-permute-start.12 = (bf16[544,384]{1,0:T(8,128)(2,1)S(1)}, bf16[544,384]{1,0:T(8,128)(2,1)}, u32[]{:S(2)}, u32[]{:S(2)}) collective-permute-start(bf16[544,384]{1,0:T(8,128)(2,1)S(1)} %get-tuple-element.185), channel_id=1, source_target_pairs={{0,8},{4,12},{8,0},{12,4},{1,9},{5,13},{9,1},{13,5},{2,10},{6,14},... | collective-permute-start | bytes 1253384 | tf_op jit(solution)/shard_map/ppermute | solution.py:568
  517.6 515.8 %all-gather.19.cloned.1.call-start = ((), (), s32[]{:S(2)}) async-start(), calls=%async_computation.2 | async-start | bytes 4177920 | tf_op jit(solution)/shard_map/all_gather | solution.py:571
  519.4 74.6 %collective-permute-start.15 = (bf16[2176,384]{1,0:T(8,128)(2,1)S(1)}, bf16[2176,384]{1,0:T(8,128)(2,1)}, u32[]{:S(2)}, u32[]{:S(2)}) collective-permute-start(bf16[2176,384]{1,0:T(8,128)(2,1)S(1)} %constant_dynamic-slice_fusion.9), channel_id=1, source_target_pairs={{0,2},{1,3},{2,0},{3,1},{4,6},{5,7},{6,4},{7,5},{8,10},{9,11},{10,... | collective-permute-start | bytes 5013512 | tf_op jit(solution)/shard_map/ppermute | solution.py:562
  593.9 33.8 %collective-permute-start.19 = (bf16[2176,768]{1,0:T(8,128)(2,1)}, bf16[2176,768]{1,0:T(8,128)(2,1)}, u32[]{:S(2)}, u32[]{:S(2)}) collective-permute-start(bf16[2176,768]{1,0:T(8,128)(2,1)} %multiply_convert_fusion.5), channel_id=1, source_target_pairs={{0,1},{1,0},{2,3},{3,2},{4,5},{5,4},{6,7},{7,6},{8,9},{9,8},{10,11... | collective-permute-start | bytes 10027016 | tf_op jit(solution)/shard_map/ppermute | solution.py:558
  597.7 20.8 %collective-permute-start.18 = (bf16[544,384]{1,0:T(8,128)(2,1)S(1)}, bf16[544,384]{1,0:T(8,128)(2,1)}, u32[]{:S(2)}, u32[]{:S(2)}) collective-permute-start(bf16[544,384]{1,0:T(8,128)(2,1)S(1)} %get-tuple-element.181), channel_id=1, source_target_pairs={{0,12},{4,8},{8,4},{12,0},{1,13},{5,9},{9,5},{13,1},{2,14},{6,10},... | collective-permute-start | bytes 1253384 | tf_op jit(solution)/shard_map/ppermute | solution.py:568
  599.2 20.6 %collective-permute-start.17 = (bf16[544,384]{1,0:T(8,128)(2,1)S(1)}, bf16[544,384]{1,0:T(8,128)(2,1)}, u32[]{:S(2)}, u32[]{:S(2)}) collective-permute-start(bf16[544,384]{1,0:T(8,128)(2,1)S(1)} %get-tuple-element.182), channel_id=1, source_target_pairs={{0,8},{4,12},{8,0},{12,4},{1,9},{5,13},{9,1},{13,5},{2,10},{6,14},... | collective-permute-start | bytes 1253384 | tf_op jit(solution)/shard_map/ppermute | solution.py:568
  622.1 415.1 %all-gather.21.cloned.1.call-start = ((), (), s32[]{:S(2)}) async-start(), calls=%async_computation.3 | async-start | bytes 4177920 | tf_op jit(solution)/shard_map/all_gather | solution.py:571
  632.0 37.9 %collective-permute-start.20 = (bf16[2176,384]{1,0:T(8,128)(2,1)S(1)}, bf16[2176,384]{1,0:T(8,128)(2,1)}, u32[]{:S(2)}, u32[]{:S(2)}) collective-permute-start(bf16[2176,384]{1,0:T(8,128)(2,1)S(1)} %constant_dynamic-slice_fusion.8), channel_id=1, source_target_pairs={{0,2},{1,3},{2,0},{3,1},{4,6},{5,7},{6,4},{7,5},{8,10},{9,11},{10,... | collective-permute-start | bytes 5013512 | tf_op jit(solution)/shard_map/ppermute | solution.py:562
  638.8 63.9 %collective-permute-start.24 = (bf16[2176,768]{1,0:T(8,128)(2,1)}, bf16[2176,768]{1,0:T(8,128)(2,1)}, u32[]{:S(2)}, u32[]{:S(2)}) collective-permute-start(bf16[2176,768]{1,0:T(8,128)(2,1)} %multiply_convert_fusion.4), channel_id=1, source_target_pairs={{0,1},{1,0},{2,3},{3,2},{4,5},{5,4},{6,7},{7,6},{8,9},{9,8},{10,11... | collective-permute-start | bytes 10027016 | tf_op jit(solution)/shard_map/ppermute | solution.py:558
  697.2 343.9 %all-gather.23.cloned.1.call-start = ((), (), s32[]{:S(2)}) async-start(), calls=%async_computation.4 | async-start | bytes 4177920 | tf_op jit(solution)/shard_map/all_gather | solution.py:571
  706.7 35.5 %collective-permute-start.25 = (bf16[2176,384]{1,0:T(8,128)(2,1)S(1)}, bf16[2176,384]{1,0:T(8,128)(2,1)}, u32[]{:S(2)}, u32[]{:S(2)}) collective-permute-start(bf16[2176,384]{1,0:T(8,128)(2,1)S(1)} %constant_dynamic-slice_fusion.7), channel_id=1, source_target_pairs={{0,2},{1,3},{2,0},{3,1},{4,6},{5,7},{6,4},{7,5},{8,10},{9,11},{10,... | collective-permute-start | bytes 5013512 | tf_op jit(solution)/shard_map/ppermute | solution.py:562
  713.5 58.1 %collective-permute-start.29 = (bf16[2176,768]{1,0:T(8,128)(2,1)}, bf16[2176,768]{1,0:T(8,128)(2,1)}, u32[]{:S(2)}, u32[]{:S(2)}) collective-permute-start(bf16[2176,768]{1,0:T(8,128)(2,1)} %multiply_convert_fusion.3), channel_id=1, source_target_pairs={{0,1},{1,0},{2,3},{3,2},{4,5},{5,4},{6,7},{7,6},{8,9},{9,8},{10,11... | collective-permute-start | bytes 10027016 | tf_op jit(solution)/shard_map/ppermute | solution.py:558
  749.0 72.8 %collective-permute-start.34 = (bf16[1536,1536]{1,0:T(8,128)(2,1)}, bf16[1536,1536]{1,0:T(8,128)(2,1)}, u32[]{:S(2)}, u32[]{:S(2)}) collective-permute-start(bf16[1536,1536]{1,0:T(8,128)(2,1)} %fusion.9), channel_id=1, source_target_pairs={{0,1},{1,0},{2,3},{3,2},{4,5},{5,4},{6,7},{7,6},{8,9},{9,8},{10,11... | collective-permute-start | bytes 14155784 | tf_op jit(solution)/shard_map/ppermute | solution.py:558
  765.9 279.1 %all-gather.25.cloned.1.call-start = ((), (), s32[]{:S(2)}) async-start(), calls=%async_computation.5 | async-start | bytes 4177920 | tf_op jit(solution)/shard_map/all_gather | solution.py:571
  777.5 30.6 %collective-permute-start.30 = (bf16[2176,384]{1,0:T(8,128)(2,1)S(1)}, bf16[2176,384]{1,0:T(8,128)(2,1)}, u32[]{:S(2)}, u32[]{:S(2)}) collective-permute-start(bf16[2176,384]{1,0:T(8,128)(2,1)S(1)} %constant_dynamic-slice_fusion.6), channel_id=1, source_target_pairs={{0,2},{1,3},{2,0},{3,1},{4,6},{5,7},{6,4},{7,5},{8,10},{9,11},{10,... | collective-permute-start | bytes 5013512 | tf_op jit(solution)/shard_map/ppermute | solution.py:562
  832.5 45.5 %collective-permute-start.35 = (bf16[768,1536]{1,0:T(8,128)(2,1)}, bf16[768,1536]{1,0:T(8,128)(2,1)}, u32[]{:S(2)}, u32[]{:S(2)}) collective-permute-start(bf16[768,1536]{1,0:T(8,128)(2,1)} %constant_dynamic-slice_fusion.3), channel_id=1, source_target_pairs={{0,2},{1,3},{2,0},{3,1},{4,6},{5,7},{6,4},{7,5},{8,10},{9,11},{10,... | collective-permute-start | bytes 7077896 | tf_op jit(solution)/shard_map/ppermute | solution.py:562
  835.3 213.5 %all-gather.27.cloned.1.call-start = ((), (), s32[]{:S(2)}) async-start(), calls=%async_computation.6 | async-start | bytes 5898240 | tf_op jit(solution)/shard_map/all_gather | solution.py:571
  853.9 62.2 %collective-permute-start.39 = (bf16[1536,1536]{1,0:T(8,128)(2,1)}, bf16[1536,1536]{1,0:T(8,128)(2,1)}, u32[]{:S(2)}, u32[]{:S(2)}) collective-permute-start(bf16[1536,1536]{1,0:T(8,128)(2,1)} %fusion.8), channel_id=1, source_target_pairs={{0,1},{1,0},{2,3},{3,2},{4,5},{5,4},{6,7},{7,6},{8,9},{9,8},{10,11... | collective-permute-start | bytes 14155784 | tf_op jit(solution)/shard_map/ppermute | solution.py:558
  882.9 21.2 %collective-permute-start.38 = (bf16[192,1536]{1,0:T(8,128)(2,1)}, bf16[192,1536]{1,0:T(8,128)(2,1)}, u32[]{:S(2)}, u32[]{:S(2)}) collective-permute-start(bf16[192,1536]{1,0:T(8,128)(2,1)} %get-tuple-element.166), channel_id=1, source_target_pairs={{0,12},{4,8},{8,4},{12,0},{1,13},{5,9},{9,5},{13,1},{2,14},{6,10},... | collective-permute-start | bytes 1769480 | tf_op jit(solution)/shard_map/ppermute | solution.py:568
  907.8 147.2 %all-gather.29.cloned.1.call-start = ((), (), s32[]{:S(2)}) async-start(), calls=%async_computation.7 | async-start | bytes 5898240 | tf_op jit(solution)/shard_map/all_gather | solution.py:571
  926.8 44.7 %collective-permute-start.40 = (bf16[768,1536]{1,0:T(8,128)(2,1)}, bf16[768,1536]{1,0:T(8,128)(2,1)}, u32[]{:S(2)}, u32[]{:S(2)}) collective-permute-start(bf16[768,1536]{1,0:T(8,128)(2,1)} %constant_dynamic-slice_fusion), channel_id=1, source_target_pairs={{0,2},{1,3},{2,0},{3,1},{4,6},{5,7},{6,4},{7,5},{8,10},{9,11},{10,... | collective-permute-start | bytes 7077896 | tf_op jit(solution)/shard_map/ppermute | solution.py:562
  929.2 50.1 %collective-permute-start = (f32[4,2,5348]{2,0,1:T(4,128)}, f32[4,2,5348]{2,0,1:T(4,128)S(1)}, u32[]{:S(2)}, u32[]{:S(2)}) collective-permute-start(f32[4,2,5348]{2,0,1:T(4,128)} %pad_maximum_fusion.17), channel_id=1, source_target_pairs={{0,1},{1,0},{2,3},{3,2},{4,5},{5,4},{6,7},{7,6},{8,9},{9,8},{10,11... | collective-permute-start | bytes 513416 | tf_op jit(solution)/shard_map/ppermute | solution.py:632
  976.2 21.0 %collective-permute-start.43 = (bf16[192,1536]{1,0:T(8,128)(2,1)}, bf16[192,1536]{1,0:T(8,128)(2,1)}, u32[]{:S(2)}, u32[]{:S(2)}) collective-permute-start(bf16[192,1536]{1,0:T(8,128)(2,1)} %get-tuple-element.169), channel_id=1, source_target_pairs={{0,12},{4,8},{8,4},{12,0},{1,13},{5,9},{9,5},{13,1},{2,14},{6,10},... | collective-permute-start | bytes 1769480 | tf_op jit(solution)/shard_map/ppermute | solution.py:568
  (108 other events, 2271.1 us)
Sparse Core Ops, SparseCore 0:
  12.3 108.1 all-gather.30
  122.0 63.2 all-gather.32
  454.7 44.1 all-gather.14
  517.7 40.8 all-gather.16
  622.2 40.8 all-gather.18
  697.3 39.8 all-gather.20
  766.0 41.1 all-gather.22
  835.4 43.3 all-gather.24
  907.9 52.2 all-gather.26
  1000.3 54.7 all-gather.28
